TPU v7x, 512 devices: a whole 4x4x16 slice. The times are simulated.
512 devices in a mesh: ka: 128 (over y, x_hi, z), col: 4 (over x_lo, core).
Axes of the slice: x: 4 (x_hi: 2, x_lo: 2; x = x_hi * 2 + x_lo), y: 4, z: 16, core: 2. Of those that a mesh axis runs over, the one named last changes fastest.
Arguments:
- amps: bfloat16 [256, 256, 192], P('ka', 'col'), may hold values from -6 to 6
- isdf_coeffs: bfloat16 [256, 2048, 256], P('ka', 'col'), may hold values from -0.375 to 0.375
- w_screen: bfloat16 [16, 2048, 2048], P(None, 'ka', 'col'), as said below
- energies: float32 [256, 256], P('ka', 'col'), may hold values from 0.5 to 3
- qsel: int32 [2], replicated, may hold values from 0 to 15
- partner: int32 [2, 256], replicated, may hold values from 0 to 255, each once within a row
Outputs:
- applied: float32 [256, 256, 192], P('ka', 'col')
Inputs may be any that keep to these rules, and one draw needn't show every extreme that they name: Each row of partner is a permutation of the 256 k points. `w_screen`: each of the 16 matrices is symmetric.
All inputs are finite; a program needn't handle non-finite values.
Results may differ from a plain program's by a relative error of at most 0.013.
Values may be sent and summed in bfloat16 or wider, within the bound.
No kernel may reach another device: no remote copies, remote signals or barrier semaphores. Data moves between devices by JAX's collectives and lax.ppermute only.
A program may use at most 64 MiB of HBM per device.

v0:
```python
import jax
import jax.numpy as jnp
from jax import lax
from jax.sharding import Mesh
from jax.sharding import PartitionSpec as P

KA = ("ka_0", "ka_1", "ka_2")


def laid_out(pieces, dim):
    lengths = list(pieces.shape[1:])
    lengths[dim] *= pieces.shape[0]
    return jnp.moveaxis(pieces, 0, dim).reshape(lengths)


def gather_in_order(array, axes, order):
    pieces = array[None]
    for k in order:
        pieces = lax.all_gather(pieces, axes[k], axis=0, tiled=True)
    carried = [lax.axis_size(axes[k]) for k in reversed(order)]
    pieces = pieces.reshape(*carried, *array.shape)
    turned = sorted(range(len(order)), key=lambda place: order[len(order) - 1 - place])
    return pieces.transpose(*turned, *range(len(order), pieces.ndim)).reshape(-1, *array.shape)


def gather_axes(array, axes, order, dim):
    return laid_out(gather_in_order(array, axes, order), dim)


def sent_to_all(array, axis):
    length = lax.axis_size(axis)
    return lax.all_to_all(
        jnp.broadcast_to(array[None], (length, *array.shape)), axis, 0, 0, tiled=True
    )


def collect(array, axis, dim):
    pieces = sent_to_all(array, axis)
    return laid_out(pieces, dim)


def split_up(array, dim, length):
    before, after = (array.shape[:dim], array.shape[dim + 1 :])
    return jnp.moveaxis(array.reshape(*before, length, -1, *after), dim, 0)


def sent_and_summed(array, axis, dim):
    pieces = split_up(array, dim, lax.axis_size(axis))
    arrived = lax.all_to_all(pieces, axis, split_axis=0, concat_axis=0, tiled=True)
    return arrived.astype(jnp.float32).sum(axis=0)


def body(amps, isdf_coeffs, w_screen, energies, qsel, partner):
    k_local = amps.shape[0]
    vectors = amps.shape[2]
    offset_base = lax.axis_index(KA) * k_local
    owned = offset_base + jnp.arange(k_local, dtype=jnp.int32)
    wanted = jnp.take(partner, owned, axis=1).reshape(-1)
    everyone = gather_axes(amps, KA, (1, 0, 2), 0)
    picked = jnp.take(everyone, wanted, axis=0)
    partners = collect(picked, "col", 1)
    partners = partners.reshape(2, k_local, partners.shape[1], vectors)
    densities = jnp.einsum(
        "kms,qkse->qmke", isdf_coeffs, partners, preferred_element_type=jnp.float32
    )
    width = densities.shape[1]
    densities = densities.astype(jnp.bfloat16).reshape(2, width, k_local * vectors)
    slabs = jnp.take(w_screen, qsel, axis=0)
    partials = jnp.einsum(
        "qrm,qmx->qrx",
        lax.all_gather(slabs, KA, axis=1, tiled=True),
        densities,
        preferred_element_type=jnp.float32,
    )
    screened = sent_and_summed(partials.astype(jnp.bfloat16), "col", 1)
    screened = screened.astype(jnp.bfloat16).reshape(2, width, k_local, vectors)
    projected = jnp.einsum(
        "kms,qmke->kse", isdf_coeffs, screened, preferred_element_type=jnp.float32
    )
    summed = sent_and_summed(projected.astype(jnp.bfloat16), "col", 1)
    return summed + energies[:, :, None] * amps.astype(jnp.float32)


def solution(mesh):
    torus = Mesh(mesh.devices.reshape(4, 2, 16, mesh.shape["col"]), ("ka_0", "ka_1", "ka_2", "col"))
    placed = (P(KA, "col", None), P(KA, "col", None), P(None, KA, "col"), P(KA, "col"), P(), P())
    return jax.shard_map(
        body, mesh=torus, in_specs=placed, out_specs=P(KA, "col", None), check_vma=False
    )
```

profile of v0, /device:TPU:1, one launch (start us, length us, event | category | flops | bytes accessed | tf_op | source)
XLA Modules:
  0.0 428.2 jit_solution(16825926341223506665)
XLA Ops:
  6.5 6.3 %all-gather = bf16[4,64,192]{2,1,0:T(8,128)(2,1)S(1)} all-gather(bf16[2,64,192]{2,1,0:T(8,128)(2,1)} %param.6), channel_id=2, replica_groups=mesh['ka_0'=4,'ka_1'=2,'ka_2'=16,'col'=4] {'ka_1'}, dimensions={0}, use_global_device_ids=true | all-gather | bytes 147456 | tf_op jit(solution)/shard_map/all_gather | solution.py:19
  12.8 11.5 %all_gather.14 = bf16[8,2,64,192]{3,2,1,0:T(8,128)(2,1)} all-gather(bf16[2,2,64,192]{3,2,1,0:T(8,128)(2,1)S(1)} %bitcast.44), channel_id=1, replica_groups=mesh['ka_0'=4,'ka_1'=2,'ka_2'=16,'col'=4] {'ka_0'}, dimensions={0}, use_global_device_ids=true | all-gather | bytes 491520 | tf_op jit(solution)/shard_map/all_gather | solution.py:19
  24.3 0.0 all-gather.6.cloned.1.call-update
  24.3 0.0 all-gather.4.cloned.1.call-start
  24.4 0.7 compare_select_fusion.4
  25.1 1.5 gather_fusion
  26.6 0.7 compare_and_fusion.2
  27.2 0.7 broadcast_select_fusion.1
  27.9 0.8 copy.48
  28.8 0.6 gather_fusion.1
  29.4 0.1 select_bitcast_fusion
  29.4 0.1 copy.49
  29.5 0.1 select_n.75
  29.6 0.1 select_n.73
  29.7 108.4 %all-gather.6.cloned.1.call-done = bf16[128,2,64,192]{3,2,1,0:T(8,128)(2,1)} async-done(((bf16[8,2,64,192]{3,2,1,0:T(8,128)(2,1)}), bf16[128,2,64,192]{3,2,1,0:T(8,128)(2,1)}) %all-gather.6.cloned.1.call-update) | async-done | bytes 6291472 | tf_op jit(solution)/shard_map/all_gather | solution.py:19
  138.1 8.3 %copy.50 = bf16[4,2,16,2,64,192]{5,4,3,2,1,0:T(8,128)(2,1)} copy(bf16[4,2,16,2,64,192]{5,4,3,1,0,2:T(8,128)(2,1)} %bitcast.37) | data formatting | bytes 12582912 | tf_op jit(solution)/shard_map/transpose | solution.py:23
  146.4 3.9 gather_fusion.2
  150.3 0.1 broadcast_select_fusion
  150.5 11.2 %all_to_all.15 = bf16[4,4,64,192]{3,2,1,0:T(8,128)(2,1)S(1)} all-to-all(bf16[4,4,64,192]{3,2,1,0:T(8,128)(2,1)S(1)} %broadcast_in_dim.45), channel_id=1, replica_groups=mesh['ka_0'=4,'ka_1'=2,'ka_2'=16,'col'=4] {'col'}, dimensions={0} | all-to-all | bytes 786432 | tf_op jit(solution)/shard_map/all_to_all | solution.py:32
  161.8 0.5 fusion
  162.3 0.1 copy.54
  162.3 192.0 %all-gather.4.cloned.1.call-done = bf16[2,2048,512]{2,1,0:T(8,128)(2,1)} async-done(((bf16[2,16,512]{2,1,0:T(8,128)(2,1)}), bf16[2,2048,512]{2,1,0:T(8,128)(2,1)}) %all-gather.4.cloned.1.call-update) | async-done | bytes 4194320 | tf_op jit(solution)/shard_map/all_gather | solution.py:71
  354.3 4.5 %convolution_convert_fusion = bf16[2,2048,384]{2,1,0:T(8,128)(2,1)S(1)} fusion(bf16[2,2048,512]{2,1,0:T(8,128)(2,1)} %all-gather.4.cloned.1.call-done, bf16[2,512,384]{1,2,0:T(8,128)(2,1)S(1)} %bitcast.43), kind=kOutput, calls=%fused_computation.3 | convolution fusion | flops 1612185600 | bytes 8126464 | tf_op jit(solution)/shard_map/qrm,qmx->qrx/dot_general | solution.py:69
  358.8 0.3 copy.67
  359.2 49.6 %all_to_all.16 = bf16[4,2,512,384]{3,2,1,0:T(8,128)(2,1)} all-to-all(bf16[4,2,512,384]{3,2,1,0:T(8,128)(2,1)S(1)} %bitcast.35), channel_id=1, replica_groups=mesh['ka_0'=4,'ka_1'=2,'ka_2'=16,'col'=4] {'col'}, dimensions={0} | all-to-all | bytes 6291456 | tf_op jit(solution)/shard_map/all_to_all | solution.py:49
  408.7 2.7 reduce_sum.32
  411.4 0.1 convert_reduce_fusion
  411.5 0.2 copy.57
  411.7 0.3 fusion.1
  412.0 0.1 copy.58
  412.2 8.4 %all_to_all.17 = bf16[4,2,64,192]{3,2,1,0:T(8,128)(2,1)S(1)} all-to-all(bf16[4,2,64,192]{3,2,1,0:T(8,128)(2,1)S(1)} %copy.59), channel_id=1, replica_groups=mesh['ka_0'=4,'ka_1'=2,'ka_2'=16,'col'=4] {'col'}, dimensions={0} | all-to-all | bytes 393216 | tf_op jit(solution)/shard_map/all_to_all | solution.py:49
  420.6 0.7 multiply_add_fusion
  (19 shorter events, 0.2 us)
Async XLA Ops:
  6.5 155.2 %copy-start = (bf16[2,512,256]{2,1,0:T(8,128)(2,1)S(1)}, bf16[2,512,256]{2,1,0:T(8,128)(2,1)}, u32[]{:S(2)}) copy-start(bf16[2,512,256]{2,1,0:T(8,128)(2,1)} %param.7) | copy-start | bytes 1572868
  6.5 131.6 %all-gather.6.cloned.1.call-start = ((), (), s32[]{:S(2)}) async-start(), calls=%async_computation.4 | async-start | bytes 8912896 | tf_op jit(solution)/shard_map/all_gather | solution.py:19
  24.3 329.9 %all-gather.4.cloned.1.call-start = ((), (), s32[]{:S(2)}) async-start(), calls=%async_computation.3 | async-start | bytes 4227072 | tf_op jit(solution)/shard_map/all_gather | solution.py:71
  408.7 11.9 %copy-start.1 = (bf16[2,64,192]{2,1,0:T(8,128)(2,1)S(1)}, bf16[2,64,192]{2,1,0:T(8,128)(2,1)}, u32[]{:S(2)}) copy-start(bf16[2,64,192]{2,1,0:T(8,128)(2,1)} %param.6) | copy-start | bytes 147460
  408.7 11.9 %copy-start.2 = (f32[2,64]{1,0:T(2,128)S(1)}, f32[2,64]{1,0:T(2,128)}, u32[]{:S(2)}) copy-start(f32[2,64]{1,0:T(2,128)} %param.9) | copy-start | bytes 1540
Sparse Core Ops, SparseCore 0:
  24.5 113.6 all-gather.5
  142.5 211.6 all-gather.3
where the time goes:
time: 429 us; the launch traced here: 428 us
  waiting for transfers between devices  300 us (70%)
  blocking collectives  87 us (20%)
  local copies, waits for them, and re-layouts  16.1 us (4%)
  between operations  13.6 us (3%)
  other arithmetic  5.77 us (1%)
  matrix products  5.3 us (1%)
    all_gather x1, waiting for transfers between devices, body(): lax.all_gather(slabs, KA, axis=1, tiled=True)  192 us
    all_gather x1, waiting for transfers between devices, gather_in_order(): pieces = lax.all_gather(pieces, axes[k], axis=0, tiled=True)  108 us
    all_to_all x2, blocking collectives, sent_and_summed(): lax.all_to_all(pieces, axis, split_axis=0, concat_axis=0, tiled=True)  58 us
    all_gather x2, blocking collectives, gather_in_order(): pieces = lax.all_gather(pieces, axes[k], axis=0, tiled=True)  17.8 us
    all_to_all x1, blocking collectives, sent_to_all(): lax.all_to_all(jnp.broadcast_to(array[None], (length, *array.shape)), axi...  11.2 us
  transfers between devices with their start and end apart: 2, of which 2 were waited for; matrix products, arithmetic and copies ran while one was open for 4% of the time, Pallas kernels for 0%

commit v1 on v0

v1 whole, which is shorter than its diff:
```python
import jax
import jax.numpy as jnp
from jax import lax
from jax.experimental import pallas as pl
from jax.experimental.pallas import tpu as pltpu
from jax.sharding import Mesh
from jax.sharding import PartitionSpec as P

KA = ("y", "xh", "z")
COL = ("xl", "c")
PLANE = ("y", "xh")
N_Y, N_XH, N_Z, N_COL = 4, 2, 16, 4
VEC = 192
SMEM = pl.BlockSpec(memory_space=pltpu.SMEM)
VMEM = pl.BlockSpec(memory_space=pltpu.VMEM)


def send_kernel(partner, place, line, out):
    z = place[1]
    for yx in range(N_Y * N_XH):
        for slot in range(4):
            wanted = partner[slot // 2, 2 * (yx * N_Z + z) + slot % 2]
            out[yx, slot] = line[wanted & 31]


def keep_kernel(partner, place, arrived, out):
    own = 2 * (place[0] * N_Z + place[1])
    for slot in range(4):
        wanted = partner[slot // 2, own + slot % 2]
        out[slot] = arrived[wanted >> 5, slot]


def by_z(block):
    rows = [block[(xh * N_Z + z) * 16 : (xh * N_Z + z + 1) * 16] for z in range(N_Z) for xh in range(N_XH)]
    return jnp.concatenate(rows, axis=0)


def density_kernel(partners, *refs):
    pieces, out = refs[:-1], refs[-1]
    turned = []
    for slot in range(4):
        whole = jnp.concatenate([partners[c, slot] for c in range(N_COL)], axis=0)
        turned.append(whole.astype(jnp.float32).T.astype(jnp.bfloat16))
    for kl in range(2):
        vectors = jnp.concatenate([turned[kl], turned[2 + kl]], axis=0)
        for i, piece in enumerate(pieces):
            dens = lax.dot_general(
                vectors, by_z(piece[kl]), (((1,), (1,)), ((), ())), preferred_element_type=jnp.float32
            ).astype(jnp.bfloat16)
            out[i, 0, kl * VEC : (kl + 1) * VEC, :] = dens[:VEC]
            out[i, 1, kl * VEC : (kl + 1) * VEC, :] = dens[VEC:]


def screen_kernel(place, w, dens, coeffs, out):
    c = place[2]
    screened = []
    for j in range(2):
        total = None
        for i in range(N_COL):
            rows = w[:, c ^ i, j].reshape(512, 512)
            part = jnp.dot(dens[i, j], rows, preferred_element_type=jnp.float32)
            total = part if total is None else total + part
        screened.append(total.astype(jnp.bfloat16))
    for kl in range(2):
        own = slice(kl * VEC, (kl + 1) * VEC)
        projected = jnp.dot(screened[0][own], coeffs[kl], preferred_element_type=jnp.float32)
        projected += jnp.dot(screened[1][own], coeffs[kl], preferred_element_type=jnp.float32)
        result = projected.T.astype(jnp.bfloat16)
        for dest in range(N_COL):
            out[dest, kl] = result[dest * 64 : (dest + 1) * 64]


def swapped(array, axis):
    return lax.ppermute(array, axis, [(0, 1), (1, 0)])


def call(kernel, shape, *args):
    specs = [SMEM if a.dtype == jnp.int32 else VMEM for a in args]
    return pl.pallas_call(
        kernel, out_shape=jax.ShapeDtypeStruct(shape, jnp.bfloat16), in_specs=specs, out_specs=VMEM
    )(*args)


def body(amps, isdf_coeffs, w_screen, energies, qsel, partner):
    place = jnp.stack([lax.axis_index(PLANE), lax.axis_index("z"), lax.axis_index(COL)]).astype(jnp.int32)
    slabs = jnp.stack([lax.dynamic_index_in_dim(w_screen, qsel[j], 0, keepdims=False) for j in range(2)])
    pair = lax.all_gather(slabs, "xh", axis=1, tiled=True)
    plane = lax.all_gather(pair, "y", axis=0, tiled=False)
    plane, amps_, coeffs_ = lax.optimization_barrier((plane, amps, isdf_coeffs))
    rows = lax.all_gather(plane, "z", axis=0, tiled=False)

    from_core = swapped(coeffs_, "c")
    from_x = swapped(coeffs_, "xl")
    from_both = swapped(from_x, "c")

    line = lax.all_gather(amps_, "z", axis=0, tiled=True)
    send = call(send_kernel, (8, 4, 64, VEC), partner, place, line)
    arrived = lax.all_to_all(send, PLANE, 0, 0, tiled=True)
    kept = call(keep_kernel, (4, 64, VEC), partner, place, arrived)
    partners = lax.all_gather(kept, COL, axis=0, tiled=False)

    dens = call(density_kernel, (4, 2, 2 * VEC, 512), partners, isdf_coeffs, from_core, from_x, from_both)
    projected = call(screen_kernel, (N_COL, 2, 64, VEC), place, rows, dens, isdf_coeffs)
    summed = lax.all_to_all(projected, COL, 0, 0, tiled=True).astype(jnp.float32).sum(axis=0)
    return summed + energies[:, :, None] * amps.astype(jnp.float32)


def solution(mesh):
    torus = Mesh(mesh.devices.reshape(N_Y, N_XH, N_Z, 2, 2), KA + COL)
    placed = (P(KA, COL, None), P(KA, COL, None), P(None, KA, COL), P(KA, COL), P(), P())
    return jax.shard_map(body, mesh=torus, in_specs=placed, out_specs=P(KA, COL, None), check_vma=False)
```

time: 429 us -> 148 us (0.34)
  waiting for transfers between devices: 300 us -> 0.03 us
  starting transfers between devices: 0.04 us -> 27.6 us
  Pallas kernels: 0 us -> 14.7 us
  local copies, waits for them, and re-layouts: 16.1 us -> 4.11 us
  matrix products: 5.3 us -> 0 us
  blocking collectives: 87 us -> 82 us
  other arithmetic: 5.77 us -> 1.41 us
    all_gather x2 -> x1, waiting for transfers between devices: 300 us -> 0.01 us  [body(): rows = lax.all_gather(plane, 'z', axis=0, tiled=False)]
    all_to_all x3 -> x1, blocking collectives: 69.2 us -> 8.5 us  [body(): lax.all_to_all(projected, COL, 0, 0, tiled=True).astype(jnp.float32)]
    all_gather x2 -> x4, blocking collectives: 17.8 us -> 73.5 us  [the longest x1 41.1 us: body(): line = lax.all_gather(amps_, 'z', axis=0, tiled=True)]
    ppermute x0 -> x3, starting transfers between devices: none -> 20.8 us  [swapped(): return lax.ppermute(array, axis, [(0, 1), (1, 0)])]
    pallas_call x0 -> x4, Pallas kernels: none -> 14.7 us  [call(): pl.pallas_call(kernel, out_shape=jax.ShapeDtypeStruct(shape, jnp.bfloat16...]
    transpose x3 -> x0, local copies, waits for them, and re-layouts: 8.31 us -> none  [the longest x1 8.25 us: gather_in_order(): pieces.transpose(*turned, *range(len(order), pieces.ndim))]
    all_to_all x0 -> x1, starting transfers between devices: none -> 6.82 us  [body(): arrived = lax.all_to_all(send, PLANE, 0, 0, tiled=True)]
    gather x3 -> x0, local copies, waits for them, and re-layouts: 5.99 us -> none  [the longest x1 3.93 us: body(): picked = jnp.take(everyone, wanted, axis=0)]
  transfers between devices with their start and end apart: 2 -> 5, of which waited for: 2 -> 0; matrix products, arithmetic and copies ran while one was open for 4% -> 0% of each run, Pallas kernels for 0% -> 6%
where the time goes in v1:
time: 148 us; the launch traced here: 147 us
  blocking collectives  82 us (55%)
  starting transfers between devices  27.6 us (19%)
  between operations  17.3 us (12%)
  Pallas kernels  14.7 us (10%)
  local copies, waits for them, and re-layouts  4.11 us (3%)
    all_gather x1, blocking collectives, body(): line = lax.all_gather(amps_, 'z', axis=0, tiled=True)  41.1 us
    ppermute x3, starting transfers between devices, swapped(): return lax.ppermute(array, axis, [(0, 1), (1, 0)])  20.8 us
    all_gather x1, blocking collectives, body(): partners = lax.all_gather(kept, COL, axis=0, tiled=False)  16.1 us
    pallas_call x4, Pallas kernels, call(): pl.pallas_call(kernel, out_shape=jax.ShapeDtypeStruct(shape, jnp.bfloat16...  14.7 us
    all_gather x1, blocking collectives, body(): plane = lax.all_gather(pair, 'y', axis=0, tiled=False)  10.8 us
    all_to_all x1, blocking collectives, body(): lax.all_to_all(projected, COL, 0, 0, tiled=True).astype(jnp.float32)  8.5 us
    all_to_all x1, starting transfers between devices, body(): arrived = lax.all_to_all(send, PLANE, 0, 0, tiled=True)  6.82 us
    all_gather x1, blocking collectives, body(): pair = lax.all_gather(slabs, 'xh', axis=1, tiled=True)  5.51 us
  transfers between devices with their start and end apart: 5, of which 0 were waited for; matrix products, arithmetic and copies ran while one was open for 0% of the time, Pallas kernels for 6%

profile of v1, /device:TPU:1, one launch (start us, length us, event | category | flops | bytes accessed | tf_op | source)
XLA Modules:
  0.0 147.3 jit_solution(4351782717969693090)
XLA Ops:
  6.5 0.0 all-gather.5.cloned.1.call-start
  6.5 1.3 fusion
  11.7 0.7 constant_dynamic-slice_fusion.1
  12.5 5.5 %all_gather.24 = bf16[2,32,512]{2,1,0:T(8,128)(2,1)S(1)} all-gather(bf16[2,16,512]{2,1,0:T(8,128)(2,1)S(1)} %pad_maximum_fusion), channel_id=1, replica_groups=mesh['y'=4,'xh'=2,'z'=16,'xl'=2,'c'=2] {'xh'}, dimensions={1}, use_global_device_ids=true | all-gather | bytes 98304 | tf_op jit(solution)/shard_map/all_gather | solution.py:87
  18.0 10.8 %all-gather = bf16[8,32,512]{2,1,0:T(8,128)(2,1)} all-gather(bf16[2,32,512]{2,1,0:T(8,128)(2,1)S(1)} %all_gather.24), channel_id=2, replica_groups=mesh['y'=4,'xh'=2,'z'=16,'xl'=2,'c'=2] {'y'}, dimensions={0}, use_global_device_ids=true | all-gather | bytes 327680 | tf_op jit(solution)/shard_map/all_gather | solution.py:88
  28.8 0.0 all-gather.5.cloned.1.call-update
  28.9 3.1 %collective-permute-start.1 = (bf16[2,512,256]{2,1,0:T(8,128)(2,1)}, bf16[2,512,256]{2,1,0:T(8,128)(2,1)S(1)}, u32[]{:S(2)}, u32[]{:S(2)}) collective-permute-start(bf16[2,512,256]{2,1,0:T(8,128)(2,1)} %coeffs.1), channel_id=1, source_target_pairs={{0,2},{2,0},{1,3},{3,1},{4,6},{6,4},{5,7},{7,5},{8,10},{10,8},{9,1... | collective-permute-start | bytes 1572872 | tf_op jit(solution)/shard_map/ppermute | solution.py:74
  32.0 41.1 %all_gather.29.line = bf16[32,64,192]{2,1,0:T(8,128)(2,1)} all-gather(bf16[2,64,192]{2,1,0:T(8,128)(2,1)} %param.6), channel_id=1, replica_groups=mesh['y'=4,'xh'=2,'z'=16,'xl'=2,'c'=2] {'z'}, dimensions={0}, use_global_device_ids=true | all-gather | bytes 835584 | tf_op jit(solution)/shard_map/all_gather | solution.py:96
  73.1 0.6 pad_add_fusion.place
  73.7 2.3 %shard_map.64 = bf16[8,4,64,192]{3,2,1,0:T(8,128)(2,1)} custom-call(s32[2,256]{1,0:T(2,128)} %partner.3, s32[3]{0:T(128)} %pad_add_fusion.place, bf16[32,64,192]{2,1,0:T(8,128)(2,1)} %all_gather.29.line), custom_call_target="tpu_custom_call" | custom-call | tf_op jit(solution)/shard_map/pallas_call | solution.py:79
  76.0 6.8 %all-to-all-start = ((bf16[8,4,64,192]{3,2,1,0:T(8,128)(2,1)}), bf16[8,4,64,192]{3,2,1,0:T(8,128)(2,1)S(1)}, u32[]{:S(2)}, u32[]{:S(2)}) async-start(bf16[8,4,64,192]{3,2,1,0:T(8,128)(2,1)} %shard_map.64), calls=%async_computation | async-start | bytes 2097152 | tf_op jit(solution)/shard_map/all_to_all | solution.py:98
  82.8 0.0 copy-done.1
  82.9 15.8 %collective-permute-start = (bf16[2,512,256]{2,1,0:T(8,128)(2,1)S(1)}, bf16[2,512,256]{2,1,0:T(8,128)(2,1)S(1)}, u32[]{:S(2)}, u32[]{:S(2)}) collective-permute-start(bf16[2,512,256]{2,1,0:T(8,128)(2,1)S(1)} %copy-done.1), channel_id=1, source_target_pairs={{0,1},{1,0},{2,3},{3,2},{4,5},{5,4},{6,7},{7,6},{8,9},{9,8},{10,11... | collective-permute-start | bytes 1572872 | tf_op jit(solution)/shard_map/ppermute | solution.py:74
  98.6 0.0 collective-permute-done.1.refs_2_
  98.6 0.0 copy-start.2
  98.6 1.9 %collective-permute-start.2 = (bf16[2,512,256]{2,1,0:T(8,128)(2,1)S(1)}, bf16[2,512,256]{2,1,0:T(8,128)(2,1)S(1)}, u32[]{:S(2)}, u32[]{:S(2)}) collective-permute-start(bf16[2,512,256]{2,1,0:T(8,128)(2,1)S(1)} %collective-permute-done.1.refs_2_), channel_id=1, source_target_pairs={{0,1},{1,0},{2,3},{3,2},{4,5},{5,4},{6,7},{7,6},{8,9},{9,8},{10,11... | collective-permute-start | bytes 1572872 | tf_op jit(solution)/shard_map/ppermute | solution.py:74
  100.6 0.0 all-to-all-done.arrived
  100.6 0.0 copy-start
  100.6 1.0 copy-done
  101.6 1.9 %shard_map.65 = bf16[4,64,192]{2,1,0:T(8,128)(2,1)} custom-call(s32[2,256]{1,0:T(2,128)} %partner.3, s32[3]{0:T(128)} %pad_add_fusion.place, bf16[8,4,64,192]{3,2,1,0:T(8,128)(2,1)} %copy-done), custom_call_target="tpu_custom_call" | custom-call | tf_op jit(solution)/shard_map/pallas_call | solution.py:79
  103.5 16.1 %all-gather.2 = bf16[16,64,192]{2,1,0:T(8,128)(2,1)} all-gather(bf16[4,64,192]{2,1,0:T(8,128)(2,1)} %shard_map.65), channel_id=4, replica_groups=mesh['y'=4,'xh'=2,'z'=16,'xl'=2,'c'=2] {'xl','c'}, dimensions={0}, use_global_device_ids=true | all-gather | bytes 491520 | tf_op jit(solution)/shard_map/all_gather | solution.py:100
  119.6 0.0 collective-permute-done.refs_1_
  119.6 0.0 collective-permute-done.2.refs_3_
  119.6 0.0 copy-start.4
  119.6 0.0 copy-done.2
  119.6 0.8 copy-done.3
  120.4 0.2 copy-done.4
  120.6 4.4 %shard_map.66.dens = bf16[4,2,384,512]{3,2,1,0:T(8,128)(2,1)} custom-call(bf16[4,4,64,192]{3,2,1,0:T(8,128)(2,1)} %bitcast.9, bf16[2,512,256]{2,1,0:T(8,128)(2,1)} %coeffs.1, bf16[2,512,256]{2,1,0:T(8,128)(2,1)} %copy-done.3, bf16[2,512,256]{2,1,0:T(8,128)(2,1)} %copy-done.2, bf16[2,512,256]{2,1,0:T(8,128)(2,1)} %copy-done.4), custom_call_target="tpu_custom_call" | custom-call | tf_op jit(solution)/shard_map/pallas_call | solution.py:79
  125.0 6.1 %shard_map.67 = bf16[4,2,64,192]{3,2,1,0:T(8,128)(2,1)} custom-call(s32[3]{0:T(128)} %pad_add_fusion.place, bf16[16,4,2,32,512]{4,3,2,1,0:T(8,128)(2,1)} %bitcast.8, bf16[4,2,384,512]{3,2,1,0:T(8,128)(2,1)} %shard_map.66.dens, bf16[2,512,256]{2,1,0:T(8,128)(2,1)} %coeffs.1), custom_call_target="tpu_custom_call" | custom-call | tf_op jit(solution)/shard_map/pallas_call | solution.py:79
  131.1 8.5 %all_to_all.10 = bf16[4,2,64,192]{3,2,1,0:T(8,128)(2,1)S(1)} all-to-all(bf16[4,2,64,192]{3,2,1,0:T(8,128)(2,1)} %shard_map.67), channel_id=1, replica_groups=mesh['y'=4,'xh'=2,'z'=16,'xl'=2,'c'=2] {'xl','c'}, dimensions={0} | all-to-all | bytes 393216 | tf_op jit(solution)/shard_map/all_to_all | solution.py:104
  139.7 0.0 copy-done.5
  139.7 0.7 multiply_add_fusion
  (8 shorter events, 0.1 us)
Async XLA Ops:
  6.5 76.3 %copy-start.1 = (bf16[2,512,256]{2,1,0:T(8,128)(2,1)S(1)}, bf16[2,512,256]{2,1,0:T(8,128)(2,1)}, u32[]{:S(2)}) copy-start(bf16[2,512,256]{2,1,0:T(8,128)(2,1)} %coeffs.1) | copy-start | bytes 1572868
  6.5 118.5 %all-gather.5.cloned.1.call-start = ((), (), s32[]{:S(2)}) async-start(), calls=%async_computation.2 | async-start | bytes 4456448 | tf_op jit(solution)/shard_map/all_gather | solution.py:90
  28.9 69.8 %collective-permute-start.1 = (bf16[2,512,256]{2,1,0:T(8,128)(2,1)}, bf16[2,512,256]{2,1,0:T(8,128)(2,1)S(1)}, u32[]{:S(2)}, u32[]{:S(2)}) collective-permute-start(bf16[2,512,256]{2,1,0:T(8,128)(2,1)} %coeffs.1), channel_id=1, source_target_pairs={{0,2},{2,0},{1,3},{3,1},{4,6},{6,4},{5,7},{7,5},{8,10},{10,8},{9,1... | collective-permute-start | bytes 1572872 | tf_op jit(solution)/shard_map/ppermute | solution.py:74
  76.0 24.5 %all-to-all-start = ((bf16[8,4,64,192]{3,2,1,0:T(8,128)(2,1)}), bf16[8,4,64,192]{3,2,1,0:T(8,128)(2,1)S(1)}, u32[]{:S(2)}, u32[]{:S(2)}) async-start(bf16[8,4,64,192]{3,2,1,0:T(8,128)(2,1)} %shard_map.64), calls=%async_computation | async-start | bytes 2097152 | tf_op jit(solution)/shard_map/all_to_all | solution.py:98
  82.9 36.7 %collective-permute-start = (bf16[2,512,256]{2,1,0:T(8,128)(2,1)S(1)}, bf16[2,512,256]{2,1,0:T(8,128)(2,1)S(1)}, u32[]{:S(2)}, u32[]{:S(2)}) collective-permute-start(bf16[2,512,256]{2,1,0:T(8,128)(2,1)S(1)} %copy-done.1), channel_id=1, source_target_pairs={{0,1},{1,0},{2,3},{3,2},{4,5},{5,4},{6,7},{7,6},{8,9},{9,8},{10,11... | collective-permute-start | bytes 1572872 | tf_op jit(solution)/shard_map/ppermute | solution.py:74
  98.6 21.0 %copy-start.2 = (bf16[2,512,256]{2,1,0:T(8,128)(2,1)}, bf16[2,512,256]{2,1,0:T(8,128)(2,1)S(1)}, u32[]{:S(2)}) copy-start(bf16[2,512,256]{2,1,0:T(8,128)(2,1)S(1)} %collective-permute-done.1.refs_2_) | copy-start | bytes 1572868
  98.6 20.9 %collective-permute-start.2 = (bf16[2,512,256]{2,1,0:T(8,128)(2,1)S(1)}, bf16[2,512,256]{2,1,0:T(8,128)(2,1)S(1)}, u32[]{:S(2)}, u32[]{:S(2)}) collective-permute-start(bf16[2,512,256]{2,1,0:T(8,128)(2,1)S(1)} %collective-permute-done.1.refs_2_), channel_id=1, source_target_pairs={{0,1},{1,0},{2,3},{3,2},{4,5},{5,4},{6,7},{7,6},{8,9},{9,8},{10,11... | collective-permute-start | bytes 1572872 | tf_op jit(solution)/shard_map/ppermute | solution.py:74
  100.6 1.0 copy-start
  119.6 0.8 copy-start.3
  119.6 1.1 copy-start.4
  125.0 14.6 %copy-start.5 = (bf16[2,64,192]{2,1,0:T(8,128)(2,1)S(1)}, bf16[2,64,192]{2,1,0:T(8,128)(2,1)}, u32[]{:S(2)}) copy-start(bf16[2,64,192]{2,1,0:T(8,128)(2,1)} %param.6) | copy-start | bytes 147460
  125.0 14.6 %copy-start.6 = (f32[2,64]{1,0:T(2,128)S(1)}, f32[2,64]{1,0:T(2,128)}, u32[]{:S(2)}) copy-start(f32[2,64]{1,0:T(2,128)} %param.9) | copy-start | bytes 1540
Sparse Core Ops, SparseCore 0:
  29.0 81.0 all-gather.4

commit v2 on v1

v2 whole, which is shorter than its diff:
```python
import jax
import jax.numpy as jnp
from jax import lax
from jax.experimental import pallas as pl
from jax.experimental.pallas import tpu as pltpu
from jax.sharding import Mesh
from jax.sharding import PartitionSpec as P

KA = ("y", "xh", "z")
COL = ("xl", "c")
PLANE = ("y", "xh")
N_Y, N_XH, N_Z, N_COL = 4, 2, 16, 4
VEC = 192
SMEM = pl.BlockSpec(memory_space=pltpu.SMEM)
VMEM = pl.BlockSpec(memory_space=pltpu.VMEM)
HBM = pl.BlockSpec(memory_space=pltpu.HBM)


def slab_kernel(qsel, w, out, arrived):
    copies = [pltpu.make_async_copy(w.at[qsel[j]], out.at[j], arrived.at[j]) for j in range(2)]
    for copy in copies:
        copy.start()
    for copy in copies:
        copy.wait()


def send_kernel(partner, line, out):
    z = lax.axis_index("z")
    for yx in range(N_Y * N_XH):
        for slot in range(4):
            wanted = partner[slot // 2, 2 * (yx * N_Z + z) + slot % 2]
            out[yx, slot] = line[wanted & 31]


def keep_kernel(partner, arrived, out):
    own = 2 * (lax.axis_index(PLANE) * N_Z + lax.axis_index("z"))
    for slot in range(4):
        wanted = partner[slot // 2, own + slot % 2]
        out[slot] = arrived[wanted >> 5, slot]


def by_z(block):
    rows = [block[(xh * N_Z + z) * 16 : (xh * N_Z + z + 1) * 16] for z in range(N_Z) for xh in range(N_XH)]
    return jnp.concatenate(rows, axis=0)


def density_kernel(partners, *refs):
    pieces, (out, coeffs, arrived) = refs[:N_COL], refs[N_COL:]
    copies = [pltpu.make_async_copy(pieces[i], coeffs.at[i], arrived.at[i]) for i in range(N_COL)]
    for copy in copies:
        copy.start()
    turned = []
    for slot in range(4):
        whole = jnp.concatenate([partners[c, slot] for c in range(N_COL)], axis=0)
        turned.append(whole.astype(jnp.float32).T.astype(jnp.bfloat16))
    vectors = [jnp.concatenate([turned[kl], turned[2 + kl]], axis=0) for kl in range(2)]
    for i in range(N_COL):
        copies[i].wait()
        for kl in range(2):
            dens = lax.dot_general(
                vectors[kl], by_z(coeffs[i, kl]), (((1,), (1,)), ((), ())), preferred_element_type=jnp.float32
            ).astype(jnp.bfloat16)
            out[i, 0, kl * VEC : (kl + 1) * VEC, :] = dens[:VEC]
            out[i, 1, kl * VEC : (kl + 1) * VEC, :] = dens[VEC:]


def screen_kernel(w, dens, own_coeffs, out, rows, coeffs, arrived, ready):
    c = lax.axis_index(COL)
    copies = [
        [pltpu.make_async_copy(w.at[:, c ^ i, j], rows.at[i, j], arrived.at[i, j]) for i in range(N_COL)]
        for j in range(2)
    ]
    for j in range(2):
        for i in range(N_COL):
            copies[j][i].start()
    last = pltpu.make_async_copy(own_coeffs, coeffs, ready)
    last.start()
    screened = []
    for j in range(2):
        total = None
        for i in range(N_COL):
            copies[j][i].wait()
            part = jnp.dot(dens[i, j], rows[i, j].reshape(512, 512), preferred_element_type=jnp.float32)
            total = part if total is None else total + part
        screened.append(total.astype(jnp.bfloat16))
    last.wait()
    for kl in range(2):
        own = slice(kl * VEC, (kl + 1) * VEC)
        projected = jnp.dot(screened[0][own], coeffs[kl], preferred_element_type=jnp.float32)
        projected += jnp.dot(screened[1][own], coeffs[kl], preferred_element_type=jnp.float32)
        result = projected.T.astype(jnp.bfloat16)
        for dest in range(N_COL):
            out[dest, kl] = result[dest * 64 : (dest + 1) * 64]


def swapped(array, axis):
    return lax.ppermute(array, axis, [(0, 1), (1, 0)])


def call(kernel, shape, specs, mib, *args, scratch=()):
    return pl.pallas_call(
        kernel,
        out_shape=jax.ShapeDtypeStruct(shape, jnp.bfloat16),
        in_specs=specs,
        out_specs=VMEM,
        scratch_shapes=scratch,
        compiler_params=pltpu.CompilerParams(vmem_limit_bytes=mib << 20),
    )(*args)


def sent_to_all(array, axis):
    length = lax.axis_size(axis)
    return lax.all_to_all(jnp.broadcast_to(array[None], (length, *array.shape)), axis, 0, 0, tiled=True)


def body(amps, isdf_coeffs, w_screen, energies, qsel, partner):
    slabs = call(
        slab_kernel, (2, 16, 512), [SMEM, HBM], 2, qsel, w_screen, scratch=[pltpu.SemaphoreType.DMA((2,))]
    )
    plane = sent_to_all(slabs, PLANE).reshape(N_Y, N_XH, 2, 16, 512).transpose(0, 2, 1, 3, 4)
    plane, amps_, coeffs_ = lax.optimization_barrier((plane, amps, isdf_coeffs))
    rows = lax.all_gather(plane.reshape(N_Y, 2, 32, 512), "z", axis=0, tiled=False)

    line = sent_to_all(amps_, "z").reshape(2 * N_Z, 64, VEC)
    from_core = swapped(coeffs_, "c")
    from_x = swapped(coeffs_, "xl")
    from_both = swapped(from_x, "c")

    send = call(send_kernel, (8, 4, 64, VEC), [SMEM, VMEM], 4, partner, line)
    arrived = lax.all_to_all(send, PLANE, 0, 0, tiled=True)
    kept = call(keep_kernel, (4, 64, VEC), [SMEM, VMEM], 4, partner, arrived)
    partners = lax.all_gather(kept, COL, axis=0, tiled=False)

    dens = call(
        density_kernel, (4, 2, 2 * VEC, 512), [VMEM] + [HBM] * N_COL, 56, partners, isdf_coeffs, from_core, from_x, from_both,
        scratch=[pltpu.VMEM((N_COL, 2, 512, 256), jnp.bfloat16), pltpu.SemaphoreType.DMA((N_COL,))],
    )
    projected = call(
        screen_kernel, (N_COL, 2, 64, VEC), [HBM, VMEM, HBM], 56, rows, dens, isdf_coeffs,
        scratch=[
            pltpu.VMEM((N_COL, 2, N_Z, 32, 512), jnp.bfloat16), pltpu.VMEM((2, 512, 256), jnp.bfloat16),
            pltpu.SemaphoreType.DMA((N_COL, 2)), pltpu.SemaphoreType.DMA,
        ],
    )
    summed = lax.all_to_all(projected, COL, 0, 0, tiled=True).astype(jnp.float32).sum(axis=0)
    return summed + energies[:, :, None] * amps.astype(jnp.float32)


def solution(mesh):
    torus = Mesh(mesh.devices.reshape(N_Y, N_XH, N_Z, 2, 2), KA + COL)
    placed = (P(KA, COL, None), P(KA, COL, None), P(None, KA, COL), P(KA, COL), P(), P())
    return jax.shard_map(body, mesh=torus, in_specs=placed, out_specs=P(KA, COL, None), check_vma=False)
```

time: 148 us -> 169 us (1.14)
  waiting for transfers between devices: 0.03 us -> 61 us
  blocking collectives: 82 us -> 43.6 us
  between operations: 17.3 us -> 13.6 us
    all_gather x3 -> x0, blocking collectives: 57.5 us -> none  [the longest x1 41.1 us: body(): line = lax.all_gather(amps_, 'z', axis=0, tiled=True)]
    all_to_all x0 -> x1, waiting for transfers between devices: none -> 53.8 us  [sent_to_all(): lax.all_to_all(jnp.broadcast_to(array[None], (length, *array.shape)), axi...]
    all_to_all x0 -> x1, blocking collectives: none -> 15.2 us  [sent_to_all(): lax.all_to_all(jnp.broadcast_to(array[None], (length, *array.shape)), axi...]
    all_to_all x0 -> x1, starting transfers between devices: none -> 14.6 us  [sent_to_all(): lax.all_to_all(jnp.broadcast_to(array[None], (length, *array.shape)), axi...]
    ppermute x3, starting transfers between devices: 20.8 us -> 10.7 us  [swapped(): return lax.ppermute(array, axis, [(0, 1), (1, 0)])]
    all_to_all x1, blocking collectives: 8.5 us -> 15.8 us  [body(): lax.all_to_all(projected, COL, 0, 0, tiled=True).astype(jnp.float32)]
    all_to_all x1, waiting for transfers between devices: 0.01 us -> 3.7 us  [body(): arrived = lax.all_to_all(send, PLANE, 0, 0, tiled=True)]
    all_gather x1, waiting for transfers between devices: 0.01 us -> 3.52 us  [body(): lax.all_gather(plane.reshape(N_Y, 2, 32, 512), 'z', axis=0, tiled=False)]
  transfers between devices with their start and end apart: 5 -> 6, of which waited for: 0 -> 3; matrix products, arithmetic and copies ran while one was open for 0% -> 1% of each run, Pallas kernels for 6% -> 5%
where the time goes in v2:
time: 169 us; the launch traced here: 168 us
  waiting for transfers between devices  61 us (36%)
  blocking collectives  43.6 us (26%)
  starting transfers between devices  28.9 us (17%)
  Pallas kernels  14.8 us (9%)
  between operations  13.6 us (8%)
  local copies, waits for them, and re-layouts  5.36 us (3%)
    all_to_all x1, waiting for transfers between devices, sent_to_all(): lax.all_to_all(jnp.broadcast_to(array[None], (length, *array.shape)), axi...  53.8 us
    all_to_all x1, blocking collectives, body(): lax.all_to_all(projected, COL, 0, 0, tiled=True).astype(jnp.float32)  15.8 us
    all_to_all x1, blocking collectives, sent_to_all(): lax.all_to_all(jnp.broadcast_to(array[None], (length, *array.shape)), axi...  15.2 us
    pallas_call x5, Pallas kernels, call(): pl.pallas_call(kernel, out_shape=jax.ShapeDtypeStruct(shape, jnp.bfloat16...  14.8 us
    all_to_all x1, starting transfers between devices, sent_to_all(): lax.all_to_all(jnp.broadcast_to(array[None], (length, *array.shape)), axi...  14.6 us
    all_gather x1, blocking collectives, body(): partners = lax.all_gather(kept, COL, axis=0, tiled=False)  12.6 us
    ppermute x3, starting transfers between devices, swapped(): return lax.ppermute(array, axis, [(0, 1), (1, 0)])  10.7 us
    all_to_all x1, waiting for transfers between devices, body(): arrived = lax.all_to_all(send, PLANE, 0, 0, tiled=True)  3.7 us
  transfers between devices with their start and end apart: 6, of which 3 were waited for; matrix products, arithmetic and copies ran while one was open for 1% of the time, Pallas kernels for 5%

profile of v2, /device:TPU:1, one launch (start us, length us, event | category | flops | bytes accessed | tf_op | source)
XLA Modules:
  0.0 168.1 jit_solution(18303605188401100423)
XLA Ops:
  6.5 0.9 copy-done
  7.5 0.7 copy-done.2
  8.1 0.6 shard_map.64
  8.8 15.2 %all_to_all.20 = bf16[8,2,16,512]{3,2,1,0:T(8,128)(2,1)S(1)} all-to-all(bf16[8,2,16,512]{3,2,1,0:T(8,128)(2,1)S(1)} %broadcast_in_dim.4), channel_id=1, replica_groups=mesh['y'=4,'xh'=2,'z'=16,'xl'=2,'c'=2] {'y','xh'}, dimensions={0} | all-to-all | bytes 524288 | tf_op jit(solution)/shard_map/all_to_all | solution.py:113
  24.0 0.7 copy.8
  24.7 0.0 all-gather.3.cloned.1.call-update
  24.7 1.9 %broadcast_in_dim.5 = bf16[16,2,64,192]{3,2,1,0:T(8,128)(2,1)} broadcast(bf16[2,64,192]{2,1,0:T(8,128)(2,1)} %param.6), dimensions={1,2,3} | broadcast | bytes 835584 | tf_op jit(solution)/shard_map/broadcast_in_dim | solution.py:113
  26.7 14.6 %all-to-all-start.1 = ((bf16[16,2,64,192]{3,2,1,0:T(8,128)(2,1)}), bf16[16,2,64,192]{3,2,1,0:T(8,128)(2,1)S(1)}, u32[]{:S(2)}, u32[]{:S(2)}) async-start(bf16[16,2,64,192]{3,2,1,0:T(8,128)(2,1)} %broadcast_in_dim.5), calls=%async_computation.1 | async-start | bytes 2097152 | tf_op jit(solution)/shard_map/all_to_all | solution.py:113
  41.3 2.2 %collective-permute-start.1 = (bf16[2,512,256]{2,1,0:T(8,128)(2,1)S(1)}, bf16[2,512,256]{2,1,0:T(8,128)(2,1)S(1)}, u32[]{:S(2)}, u32[]{:S(2)}) collective-permute-start(bf16[2,512,256]{2,1,0:T(8,128)(2,1)S(1)} %copy-done.3), channel_id=1, source_target_pairs={{0,2},{2,0},{1,3},{3,1},{4,6},{6,4},{5,7},{7,5},{8,10},{10,8},{9,1... | collective-permute-start | bytes 1572872 | tf_op jit(solution)/shard_map/ppermute | solution.py:97
  43.6 53.8 %all-to-all-done.1 = bf16[16,2,64,192]{3,2,1,0:T(8,128)(2,1)S(1)} async-done(((bf16[16,2,64,192]{3,2,1,0:T(8,128)(2,1)}), bf16[16,2,64,192]{3,2,1,0:T(8,128)(2,1)S(1)}, u32[]{:S(2)}, u32[]{:S(2)}) %all-to-all-start.1) | async-done | bytes 786464 | tf_op jit(solution)/shard_map/all_to_all | solution.py:113
  97.4 0.0 copy-done.1
  97.4 1.6 shard_map.65
  99.0 3.6 %all-to-all-start.2 = ((bf16[8,4,64,192]{3,2,1,0:T(8,128)(2,1)}), bf16[8,4,64,192]{3,2,1,0:T(8,128)(2,1)S(1)}, u32[]{:S(2)}, u32[]{:S(2)}) async-start(bf16[8,4,64,192]{3,2,1,0:T(8,128)(2,1)} %shard_map.65), calls=%async_computation.2 | async-start | bytes 2097152 | tf_op jit(solution)/shard_map/all_to_all | solution.py:130
  102.6 6.6 %collective-permute-start = (bf16[2,512,256]{2,1,0:T(8,128)(2,1)S(1)}, bf16[2,512,256]{2,1,0:T(8,128)(2,1)S(1)}, u32[]{:S(2)}, u32[]{:S(2)}) collective-permute-start(bf16[2,512,256]{2,1,0:T(8,128)(2,1)S(1)} %copy-done.3), channel_id=1, source_target_pairs={{0,1},{1,0},{2,3},{3,2},{4,5},{5,4},{6,7},{7,6},{8,9},{9,8},{10,11... | collective-permute-start | bytes 1572872 | tf_op jit(solution)/shard_map/ppermute | solution.py:97
  109.2 0.0 collective-permute-done.1.refs_2_
  109.2 0.0 copy-start.4
  109.2 1.9 %collective-permute-start.2 = (bf16[2,512,256]{2,1,0:T(8,128)(2,1)S(1)}, bf16[2,512,256]{2,1,0:T(8,128)(2,1)S(1)}, u32[]{:S(2)}, u32[]{:S(2)}) collective-permute-start(bf16[2,512,256]{2,1,0:T(8,128)(2,1)S(1)} %collective-permute-done.1.refs_2_), channel_id=1, source_target_pairs={{0,1},{1,0},{2,3},{3,2},{4,5},{5,4},{6,7},{7,6},{8,9},{9,8},{10,11... | collective-permute-start | bytes 1572872 | tf_op jit(solution)/shard_map/ppermute | solution.py:97
  111.1 3.7 %all-to-all-done.2.arrived = bf16[8,4,64,192]{3,2,1,0:T(8,128)(2,1)S(1)} async-done(((bf16[8,4,64,192]{3,2,1,0:T(8,128)(2,1)}), bf16[8,4,64,192]{3,2,1,0:T(8,128)(2,1)S(1)}, u32[]{:S(2)}, u32[]{:S(2)}) %all-to-all-start.2) | async-done | bytes 786464 | tf_op jit(solution)/shard_map/all_to_all | solution.py:130
  114.8 0.6 shard_map.66
  115.4 12.6 %all-gather = bf16[16,64,192]{2,1,0:T(8,128)(2,1)} all-gather(bf16[4,64,192]{2,1,0:T(8,128)(2,1)S(1)} %shard_map.66), channel_id=2, replica_groups=mesh['y'=4,'xh'=2,'z'=16,'xl'=2,'c'=2] {'xl','c'}, dimensions={0}, use_global_device_ids=true | all-gather | bytes 491520 | tf_op jit(solution)/shard_map/all_gather | solution.py:132
  128.0 0.0 collective-permute-done.refs_1_
  128.0 0.0 collective-permute-done.2.refs_3_
  128.1 0.0 copy-start.6
  128.1 0.8 copy-done.5
  128.9 0.2 copy-done.6
  129.1 5.4 %shard_map.67.dens = bf16[4,2,384,512]{3,2,1,0:T(8,128)(2,1)} custom-call(bf16[4,4,64,192]{3,2,1,0:T(8,128)(2,1)} %bitcast.7, bf16[2,512,256]{2,1,0:T(8,128)(2,1)} %own_coeffs.1, bf16[2,512,256]{2,1,0:T(8,128)(2,1)} %copy-done.5, bf16[2,512,256]{2,1,0:T(8,128)(2,1)} %copy-done.4, bf16[2,512,256]{2,1,0:T(8,128)(2,1)} %copy-done.6), custom_call_target="tpu_custom_call" | custom-call | tf_op jit(solution)/shard_map/pallas_call | solution.py:101
  134.5 0.0 copy-start.7
  134.5 0.0 copy-start.8
  134.6 3.5 %all-gather.3.cloned.1.call-done.w = bf16[16,4,2,32,512]{4,3,2,1,0:T(8,128)(2,1)} async-done(((bf16[1,4,2,32,512]{4,3,2,1,0:T(8,128)(2,1)}), bf16[16,4,2,32,512]{4,3,2,1,0:T(8,128)(2,1)}) %all-gather.3.cloned.1.call-update) | async-done | bytes 4194320 | tf_op jit(solution)/shard_map/all_gather | solution.py:122
  138.1 6.6 %shard_map.68 = bf16[4,2,64,192]{3,2,1,0:T(8,128)(2,1)} custom-call(bf16[16,4,2,32,512]{4,3,2,1,0:T(8,128)(2,1)} %all-gather.3.cloned.1.call-done.w, bf16[4,2,384,512]{3,2,1,0:T(8,128)(2,1)} %shard_map.67.dens, bf16[2,512,256]{2,1,0:T(8,128)(2,1)} %own_coeffs.1), custom_call_target="tpu_custom_call" | custom-call | tf_op jit(solution)/shard_map/pallas_call | solution.py:101
  144.7 15.8 %all_to_all.21 = bf16[4,2,64,192]{3,2,1,0:T(8,128)(2,1)S(1)} all-to-all(bf16[4,2,64,192]{3,2,1,0:T(8,128)(2,1)} %shard_map.68), channel_id=1, replica_groups=mesh['y'=4,'xh'=2,'z'=16,'xl'=2,'c'=2] {'xl','c'}, dimensions={0} | all-to-all | bytes 393216 | tf_op jit(solution)/shard_map/all_to_all | solution.py:145
  160.5 0.7 multiply_add_fusion
  (12 shorter events, 0.1 us)
Async XLA Ops:
  6.5 131.5 %all-gather.3.cloned.1.call-start = ((), (), s32[]{:S(2)}) async-start(), calls=%async_computation.4 | async-start | bytes 4456448 | tf_op jit(solution)/shard_map/all_gather | solution.py:122
  6.5 0.9 copy-start
  7.5 0.7 copy-start.2
  8.1 33.2 %copy-start.3 = (bf16[2,512,256]{2,1,0:T(8,128)(2,1)S(1)}, bf16[2,512,256]{2,1,0:T(8,128)(2,1)}, u32[]{:S(2)}) copy-start(bf16[2,512,256]{2,1,0:T(8,128)(2,1)} %own_coeffs.1) | copy-start | bytes 1572868
  8.1 89.2 %copy-start.1 = (s32[2,256]{1,0:T(2,128)S(1)}, s32[2,256]{1,0:T(2,128)}, u32[]{:S(2)}) copy-start(s32[2,256]{1,0:T(2,128)} %partner.3) | copy-start | bytes 6148
  26.7 70.7 %all-to-all-start.1 = ((bf16[16,2,64,192]{3,2,1,0:T(8,128)(2,1)}), bf16[16,2,64,192]{3,2,1,0:T(8,128)(2,1)S(1)}, u32[]{:S(2)}, u32[]{:S(2)}) async-start(bf16[16,2,64,192]{3,2,1,0:T(8,128)(2,1)} %broadcast_in_dim.5), calls=%async_computation.1 | async-start | bytes 2097152 | tf_op jit(solution)/shard_map/all_to_all | solution.py:113
  41.3 67.8 %collective-permute-start.1 = (bf16[2,512,256]{2,1,0:T(8,128)(2,1)S(1)}, bf16[2,512,256]{2,1,0:T(8,128)(2,1)S(1)}, u32[]{:S(2)}, u32[]{:S(2)}) collective-permute-start(bf16[2,512,256]{2,1,0:T(8,128)(2,1)S(1)} %copy-done.3), channel_id=1, source_target_pairs={{0,2},{2,0},{1,3},{3,1},{4,6},{6,4},{5,7},{7,5},{8,10},{10,8},{9,1... | collective-permute-start | bytes 1572872 | tf_op jit(solution)/shard_map/ppermute | solution.py:97
  99.0 15.8 %all-to-all-start.2 = ((bf16[8,4,64,192]{3,2,1,0:T(8,128)(2,1)}), bf16[8,4,64,192]{3,2,1,0:T(8,128)(2,1)S(1)}, u32[]{:S(2)}, u32[]{:S(2)}) async-start(bf16[8,4,64,192]{3,2,1,0:T(8,128)(2,1)} %shard_map.65), calls=%async_computation.2 | async-start | bytes 2097152 | tf_op jit(solution)/shard_map/all_to_all | solution.py:130
  102.6 25.5 %collective-permute-start = (bf16[2,512,256]{2,1,0:T(8,128)(2,1)S(1)}, bf16[2,512,256]{2,1,0:T(8,128)(2,1)S(1)}, u32[]{:S(2)}, u32[]{:S(2)}) collective-permute-start(bf16[2,512,256]{2,1,0:T(8,128)(2,1)S(1)} %copy-done.3), channel_id=1, source_target_pairs={{0,1},{1,0},{2,3},{3,2},{4,5},{5,4},{6,7},{7,6},{8,9},{9,8},{10,11... | collective-permute-start | bytes 1572872 | tf_op jit(solution)/shard_map/ppermute | solution.py:97
  109.2 18.9 %copy-start.4 = (bf16[2,512,256]{2,1,0:T(8,128)(2,1)}, bf16[2,512,256]{2,1,0:T(8,128)(2,1)S(1)}, u32[]{:S(2)}) copy-start(bf16[2,512,256]{2,1,0:T(8,128)(2,1)S(1)} %collective-permute-done.1.refs_2_) | copy-start | bytes 1572868
  109.2 18.9 %collective-permute-start.2 = (bf16[2,512,256]{2,1,0:T(8,128)(2,1)S(1)}, bf16[2,512,256]{2,1,0:T(8,128)(2,1)S(1)}, u32[]{:S(2)}, u32[]{:S(2)}) collective-permute-start(bf16[2,512,256]{2,1,0:T(8,128)(2,1)S(1)} %collective-permute-done.1.refs_2_), channel_id=1, source_target_pairs={{0,1},{1,0},{2,3},{3,2},{4,5},{5,4},{6,7},{7,6},{8,9},{9,8},{10,11... | collective-permute-start | bytes 1572872 | tf_op jit(solution)/shard_map/ppermute | solution.py:97
  128.0 0.8 copy-start.5
  128.1 1.1 copy-start.6
  134.5 25.9 %copy-start.7 = (bf16[2,64,192]{2,1,0:T(8,128)(2,1)S(1)}, bf16[2,64,192]{2,1,0:T(8,128)(2,1)}, u32[]{:S(2)}) copy-start(bf16[2,64,192]{2,1,0:T(8,128)(2,1)} %param.6) | copy-start | bytes 147460
  134.5 25.9 %copy-start.8 = (f32[2,64]{1,0:T(2,128)S(1)}, f32[2,64]{1,0:T(2,128)}, u32[]{:S(2)}) copy-start(f32[2,64]{1,0:T(2,128)} %param.9) | copy-start | bytes 1540
Sparse Core Ops, SparseCore 0:
  24.9 113.1 all-gather.2

commit v3 on v2

v3 whole, which is shorter than its diff:
```python
import jax
import jax.numpy as jnp
from jax import lax
from jax.experimental import pallas as pl
from jax.experimental.pallas import tpu as pltpu
from jax.sharding import Mesh
from jax.sharding import PartitionSpec as P


KA = ("y", "xh", "z")
COL = ("xl", "c")
PLANE = ("y", "xh")
N_Y, N_XH, N_Z, N_COL = 4, 2, 16, 4
VEC = 192
SMEM = pl.BlockSpec(memory_space=pltpu.SMEM)
VMEM = pl.BlockSpec(memory_space=pltpu.VMEM)
HBM = pl.BlockSpec(memory_space=pltpu.HBM)


def slab_kernel(qsel, w, out, arrived):
    copies = [pltpu.make_async_copy(w.at[qsel[j]], out.at[j], arrived.at[j]) for j in range(2)]
    for copy in copies:
        copy.start()
    for copy in copies:
        copy.wait()


def joined(first, second, half):
    top = lax.broadcasted_iota(jnp.int32, first.shape, 0) < 4
    return jnp.where(top, turned(first, half[0] == 1), turned(second, half[1] == 0))


def turned(tile, swap):
    other = pltpu.roll(tile, 4, 0)
    if isinstance(swap, bool):
        return other if swap else tile
    return jnp.where(swap, other, tile)


def spread_kernel(amps, out):
    for q in range(8):
        own = [amps[kl, 8 * q : 8 * q + 8].astype(jnp.float32) for kl in range(2)]
        for half in range(2):
            out[2 * q + half] = joined(own[0], own[1], (half, half)).astype(jnp.bfloat16)


def send_kernel(partner, held, out):
    base = 2 * N_Z * lax.axis_index(PLANE)
    for z in range(N_Z):
        for j in range(2):
            wanted = [partner[j, base + 2 * z + kl] for kl in range(2)]
            tiles = [held[p >> 5, (p >> 1) & 15].astype(jnp.float32) for p in wanted]
            out[z, j] = joined(tiles[0], tiles[1], (wanted[0] & 1, wanted[1] & 1)).astype(jnp.bfloat16)


def keep_kernel(arrived, out):
    for j in range(2):
        for q in range(8):
            tiles = [arrived[2 * q + half, j].astype(jnp.float32) for half in range(2)]
            for kl in range(2):
                out[2 * j + kl, 8 * q : 8 * q + 8] = joined(tiles[0], tiles[1], (kl, kl)).astype(jnp.bfloat16)


def by_z(block):
    rows = [block[(xh * N_Z + z) * 16 : (xh * N_Z + z + 1) * 16] for z in range(N_Z) for xh in range(N_XH)]
    return jnp.concatenate(rows, axis=0)


def density_kernel(partners, *refs):
    pieces, (out, coeffs, dens, arrived, written) = refs[:N_COL], refs[N_COL:]
    copies = [pltpu.make_async_copy(pieces[i], coeffs.at[i], arrived.at[i]) for i in range(N_COL)]
    stores = [pltpu.make_async_copy(dens.at[i], out.at[i], written.at[i]) for i in range(N_COL)]
    for copy in copies:
        copy.start()
    columns = []
    for slot in range(4):
        whole = jnp.concatenate([partners[c, slot] for c in range(N_COL)], axis=0)
        columns.append(whole.astype(jnp.float32).T.astype(jnp.bfloat16))
    vectors = [jnp.concatenate([columns[kl], columns[2 + kl]], axis=0) for kl in range(2)]
    for i in range(N_COL):
        copies[i].wait()
        for kl in range(2):
            part = lax.dot_general(
                vectors[kl], by_z(coeffs[i, kl]), (((1,), (1,)), ((), ())), preferred_element_type=jnp.float32
            ).astype(jnp.bfloat16)
            dens[i, 0, kl * VEC : (kl + 1) * VEC, :] = part[:VEC]
            dens[i, 1, kl * VEC : (kl + 1) * VEC, :] = part[VEC:]
        stores[i].start()
    for store in stores:
        store.wait()


def screen_kernel(w, dens, own_coeffs, out, rows, held, coeffs, arrived, fetched, ready):
    c = lax.axis_index(COL)
    steps = [(j, i) for j in range(2) for i in range(N_COL)]
    copies = {(j, i): pltpu.make_async_copy(w.at[:, c ^ i, :, j], rows.at[i, j], arrived.at[i, j]) for j, i in steps}
    fetches = {(j, i): pltpu.make_async_copy(dens.at[i, j], held.at[i, j], fetched.at[i, j]) for j, i in steps}
    for step in steps:
        fetches[step].start()
        copies[step].start()
    last = pltpu.make_async_copy(own_coeffs, coeffs, ready)
    last.start()
    screened = []
    for j in range(2):
        total = None
        for i in range(N_COL):
            fetches[j, i].wait()
            copies[j, i].wait()
            part = jnp.dot(held[i, j], rows[i, j].reshape(512, 512), preferred_element_type=jnp.float32)
            total = part if total is None else total + part
        screened.append(total.astype(jnp.bfloat16))
    last.wait()
    for kl in range(2):
        own = slice(kl * VEC, (kl + 1) * VEC)
        projected = jnp.dot(screened[0][own], coeffs[kl], preferred_element_type=jnp.float32)
        projected += jnp.dot(screened[1][own], coeffs[kl], preferred_element_type=jnp.float32)
        result = projected.T.astype(jnp.bfloat16)
        for dest in range(N_COL):
            out[dest, kl] = result[dest * 64 : (dest + 1) * 64]


def swapped(array, axis):
    return lax.ppermute(array, axis, [(0, 1), (1, 0)])


def call(kernel, shape, specs, mib, *args, scratch=(), out=VMEM):
    return pl.pallas_call(
        kernel,
        out_shape=jax.ShapeDtypeStruct(shape, jnp.bfloat16),
        in_specs=specs,
        out_specs=out,
        scratch_shapes=scratch,
        compiler_params=pltpu.CompilerParams(vmem_limit_bytes=mib << 20),
    )(*args)


def sent_to_all(array, axis):
    length = lax.axis_size(axis)
    return lax.all_to_all(jnp.broadcast_to(array[None], (length, *array.shape)), axis, 0, 0, tiled=True)


def body(amps, isdf_coeffs, w_screen, energies, qsel, partner):
    pieces = call(spread_kernel, (N_Z, 8, VEC), [VMEM], 4, amps)
    spread = lax.all_to_all(pieces, "z", 0, 0, tiled=True)
    slabs = call(
        slab_kernel, (2, 16, 512), [SMEM, HBM], 60, qsel, w_screen, scratch=[pltpu.SemaphoreType.DMA((2,))]
    )
    plane = lax.all_gather(lax.all_gather(slabs, "xh", axis=0, tiled=False), "y", axis=0, tiled=False)
    plane, coeffs = lax.optimization_barrier((plane, isdf_coeffs))
    rows = lax.all_gather(plane.reshape(N_Y, N_XH, 2, 16, 512), "z", axis=0, tiled=False)

    held = sent_to_all(spread, PLANE)
    from_core = swapped(coeffs, "c")
    from_x = swapped(coeffs, "xl")
    from_both = swapped(from_x, "c")

    send = call(send_kernel, (N_Z, 2, 8, VEC), [SMEM, VMEM], 4, partner, held)
    arrived = lax.all_to_all(send, "z", 0, 0, tiled=True)
    kept = call(keep_kernel, (4, 64, VEC), [VMEM], 4, arrived)
    partners = lax.all_gather(kept, COL, axis=0, tiled=False)

    dens = call(
        density_kernel, (N_COL, 2, 2 * VEC, 512), [VMEM] + [HBM] * N_COL, 57,
        partners, isdf_coeffs, from_core, from_x, from_both, out=HBM,
        scratch=[
            pltpu.VMEM((N_COL, 2, 512, 256), jnp.bfloat16), pltpu.VMEM((N_COL, 2, 2 * VEC, 512), jnp.bfloat16),
            pltpu.SemaphoreType.DMA((N_COL,)), pltpu.SemaphoreType.DMA((N_COL,)),
        ],
    )
    projected = call(
        screen_kernel, (N_COL, 2, 64, VEC), [HBM] * 3, 60, rows, dens, isdf_coeffs,
        scratch=[
            pltpu.VMEM((N_COL, 2, N_Z, N_XH, 16, 512), jnp.bfloat16),
            pltpu.VMEM((N_COL, 2, 2 * VEC, 512), jnp.bfloat16), pltpu.VMEM((2, 512, 256), jnp.bfloat16),
            pltpu.SemaphoreType.DMA((N_COL, 2)), pltpu.SemaphoreType.DMA((N_COL, 2)), pltpu.SemaphoreType.DMA,
        ],
    )
    summed = lax.all_to_all(projected, COL, 0, 0, tiled=True).astype(jnp.float32).sum(axis=0)
    return summed + energies[:, :, None] * amps.astype(jnp.float32)


def solution(mesh):
    torus = Mesh(mesh.devices.reshape(N_Y, N_XH, N_Z, 2, 2), KA + COL)
    placed = (P(KA, COL, None), P(KA, COL, None), P(None, KA, COL), P(KA, COL), P(), P())
    return jax.shard_map(body, mesh=torus, in_specs=placed, out_specs=P(KA, COL, None), check_vma=False)
```

time: 169 us -> 139 us (0.82)
  waiting for transfers between devices: 61 us -> 0.05 us
  blocking collectives: 43.6 us -> 88.3 us
  starting transfers between devices: 28.9 us -> 19.5 us
  Pallas kernels: 14.8 us -> 12.6 us
  local copies, waits for them, and re-layouts: 5.36 us -> 3.39 us
    all_to_all x1, waiting for transfers between devices: 53.8 us -> 0.01 us  [sent_to_all(): lax.all_to_all(jnp.broadcast_to(array[None], (length, *array.shape)), axi...]
    all_to_all x1 -> x2, blocking collectives: 15.2 us -> 41.8 us  [the longest x1 26.4 us: body(): spread = lax.all_to_all(pieces, 'z', 0, 0, tiled=True)]
    all_gather x0 -> x2, blocking collectives: none -> 16.6 us  [the longest x1 10.8 us: body(): lax.all_gather(lax.all_gather(slabs, 'xh', axis=0, tiled=False), 'y', axi...]
    all_to_all x1, starting transfers between devices: 14.6 us -> 5.67 us  [sent_to_all(): lax.all_to_all(jnp.broadcast_to(array[None], (length, *array.shape)), axi...]
    all_to_all x1 -> x0, waiting for transfers between devices: 3.7 us -> none  [body(): arrived = lax.all_to_all(send, PLANE, 0, 0, tiled=True)]
    all_to_all x1 -> x0, starting transfers between devices: 3.56 us -> none  [body(): arrived = lax.all_to_all(send, PLANE, 0, 0, tiled=True)]
    all_gather x1, waiting for transfers between devices: 3.52 us -> 0.02 us  [body(): lax.all_gather(plane.reshape(N_Y, N_XH, 2, 16, 512), 'z', axis=0, tiled=F...]
    ppermute x3, starting transfers between devices: 10.7 us -> 13.8 us  [swapped(): return lax.ppermute(array, axis, [(0, 1), (1, 0)])]
  transfers between devices with their start and end apart: 6 -> 5, of which waited for: 3 -> 0; matrix products, arithmetic and copies ran while one was open for 1% -> 1% of each run, Pallas kernels for 5% -> 4%
where the time goes in v3:
time: 139 us; the launch traced here: 138 us
  blocking collectives  88.3 us (64%)
  starting transfers between devices  19.5 us (14%)
  between operations  13.6 us (10%)
  Pallas kernels  12.6 us (9%)
  local copies, waits for them, and re-layouts  3.39 us (2%)
    all_to_all x1, blocking collectives, body(): spread = lax.all_to_all(pieces, 'z', 0, 0, tiled=True)  26.4 us
    all_to_all x1, blocking collectives, body(): lax.all_to_all(projected, COL, 0, 0, tiled=True).astype(jnp.float32)  15.5 us
    all_to_all x1, blocking collectives, body(): arrived = lax.all_to_all(send, 'z', 0, 0, tiled=True)  15.5 us
    all_gather x1, blocking collectives, body(): partners = lax.all_gather(kept, COL, axis=0, tiled=False)  14.4 us
    ppermute x3, starting transfers between devices, swapped(): return lax.ppermute(array, axis, [(0, 1), (1, 0)])  13.8 us
    pallas_call x6, Pallas kernels, call(): pl.pallas_call(kernel, out_shape=jax.ShapeDtypeStruct(shape, jnp.bfloat16...  12.6 us
    all_gather x1, blocking collectives, body(): lax.all_gather(lax.all_gather(slabs, 'xh', axis=0, tiled=False), 'y', axi...  10.8 us
    all_gather x1, blocking collectives, body(): lax.all_gather(slabs, 'xh', axis=0, tiled=False)  5.8 us
  transfers between devices with their start and end apart: 5, of which 0 were waited for; matrix products, arithmetic and copies ran while one was open for 1% of the time, Pallas kernels for 4%

profile of v3, /device:TPU:1, one launch (start us, length us, event | category | flops | bytes accessed | tf_op | source)
XLA Modules:
  0.0 138.3 jit_solution(4490725182112595216)
XLA Ops:
  6.5 2.0 %shard_map.64 = bf16[2,16,512]{2,1,0:T(8,128)(2,1)} custom-call(s32[2]{0:T(128)} %qsel.1, bf16[16,16,512]{2,1,0:T(8,128)(2,1)} %w.1), custom_call_target="tpu_custom_call" | custom-call | tf_op jit(solution)/shard_map/pallas_call | solution.py:127
  8.6 5.8 %all-gather = bf16[4,16,512]{2,1,0:T(8,128)(2,1)S(1)} all-gather(bf16[2,16,512]{2,1,0:T(8,128)(2,1)} %shard_map.64), channel_id=2, replica_groups=mesh['y'=4,'xh'=2,'z'=16,'xl'=2,'c'=2] {'xh'}, dimensions={0}, use_global_device_ids=true | all-gather | bytes 98304 | tf_op jit(solution)/shard_map/all_gather | solution.py:148
  14.4 10.8 %all-gather.1 = bf16[8,2,16,512]{3,2,1,0:T(8,128)(2,1)} all-gather(bf16[2,2,16,512]{3,2,1,0:T(8,128)(2,1)S(1)} %bitcast.7), channel_id=3, replica_groups=mesh['y'=4,'xh'=2,'z'=16,'xl'=2,'c'=2] {'y'}, dimensions={0}, use_global_device_ids=true | all-gather | bytes 327680 | tf_op jit(solution)/shard_map/all_gather | solution.py:148
  25.2 0.0 all-gather.6.cloned.1.call-update
  25.2 3.1 %collective-permute-start.1 = (bf16[2,512,256]{2,1,0:T(8,128)(2,1)}, bf16[2,512,256]{2,1,0:T(8,128)(2,1)S(1)}, u32[]{:S(2)}, u32[]{:S(2)}) collective-permute-start(bf16[2,512,256]{2,1,0:T(8,128)(2,1)} %own_coeffs.1), channel_id=1, source_target_pairs={{0,2},{2,0},{1,3},{3,1},{4,6},{6,4},{5,7},{7,5},{8,10},{10,8},{9,1... | collective-permute-start | bytes 1572872 | tf_op jit(solution)/shard_map/ppermute | solution.py:123
  28.3 0.0 copy-start
  28.3 0.8 copy-done
  29.2 26.4 %all_to_all.20 = bf16[16,8,192]{2,1,0:T(8,128)(2,1)S(1)} all-to-all(bf16[16,8,192]{2,1,0:T(8,128)(2,1)S(1)} %shard_map.65), channel_id=1, replica_groups=mesh['y'=4,'xh'=2,'z'=16,'xl'=2,'c'=2] {'z'}, dimensions={0} | all-to-all | bytes 98304 | tf_op jit(solution)/shard_map/all_to_all | solution.py:144
  55.5 0.8 broadcast_in_dim.2
  56.4 5.7 %all-to-all-start.1 = ((bf16[8,16,8,192]{3,2,1,0:T(8,128)(2,1)}), bf16[8,16,8,192]{3,2,1,0:T(8,128)(2,1)S(1)}, u32[]{:S(2)}, u32[]{:S(2)}) async-start(bf16[8,16,8,192]{3,2,1,0:T(8,128)(2,1)} %broadcast_in_dim.2), calls=%async_computation.1 | async-start | bytes 1048576 | tf_op jit(solution)/shard_map/all_to_all | solution.py:139
  62.0 8.8 %collective-permute-start = (bf16[2,512,256]{2,1,0:T(8,128)(2,1)}, bf16[2,512,256]{2,1,0:T(8,128)(2,1)S(1)}, u32[]{:S(2)}, u32[]{:S(2)}) collective-permute-start(bf16[2,512,256]{2,1,0:T(8,128)(2,1)} %own_coeffs.1), channel_id=1, source_target_pairs={{0,1},{1,0},{2,3},{3,2},{4,5},{5,4},{6,7},{7,6},{8,9},{9,8},{10,11... | collective-permute-start | bytes 1572872 | tf_op jit(solution)/shard_map/ppermute | solution.py:123
  70.9 0.0 collective-permute-done.1.refs_2_
  70.9 1.9 %collective-permute-start.2 = (bf16[2,512,256]{2,1,0:T(8,128)(2,1)S(1)}, bf16[2,512,256]{2,1,0:T(8,128)(2,1)S(1)}, u32[]{:S(2)}, u32[]{:S(2)}) collective-permute-start(bf16[2,512,256]{2,1,0:T(8,128)(2,1)S(1)} %collective-permute-done.1.refs_2_), channel_id=1, source_target_pairs={{0,1},{1,0},{2,3},{3,2},{4,5},{5,4},{6,7},{7,6},{8,9},{9,8},{10,11... | collective-permute-start | bytes 1572872 | tf_op jit(solution)/shard_map/ppermute | solution.py:123
  72.8 0.0 all-to-all-done.1.held
  72.8 0.0 copy-start.2
  72.8 0.7 copy-done.2
  73.5 0.8 shard_map.66
  74.3 15.5 %all_to_all.21.arrived = bf16[16,2,8,192]{3,2,1,0:T(8,128)(2,1)S(1)} all-to-all(bf16[16,2,8,192]{3,2,1,0:T(8,128)(2,1)S(1)} %shard_map.66), channel_id=1, replica_groups=mesh['y'=4,'xh'=2,'z'=16,'xl'=2,'c'=2] {'z'}, dimensions={0} | all-to-all | bytes 196608 | tf_op jit(solution)/shard_map/all_to_all | solution.py:158
  89.8 14.4 %all-gather.3 = bf16[16,64,192]{2,1,0:T(8,128)(2,1)} all-gather(bf16[4,64,192]{2,1,0:T(8,128)(2,1)S(1)} %shard_map.67), channel_id=5, replica_groups=mesh['y'=4,'xh'=2,'z'=16,'xl'=2,'c'=2] {'xl','c'}, dimensions={0}, use_global_device_ids=true | all-gather | bytes 491520 | tf_op jit(solution)/shard_map/all_gather | solution.py:160
  104.2 0.0 collective-permute-done.refs_1_
  104.2 0.0 collective-permute-done.2.refs_3_
  104.3 0.8 copy-done.4
  105.1 0.2 copy-done.5
  105.3 4.7 %shard_map.68.dens = bf16[4,2,384,512]{3,2,1,0:T(8,128)(2,1)} custom-call(bf16[4,4,64,192]{3,2,1,0:T(8,128)(2,1)} %bitcast.5, bf16[2,512,256]{2,1,0:T(8,128)(2,1)} %own_coeffs.1, bf16[2,512,256]{2,1,0:T(8,128)(2,1)} %copy-done.4, bf16[2,512,256]{2,1,0:T(8,128)(2,1)} %copy-done.3, bf16[2,512,256]{2,1,0:T(8,128)(2,1)} %copy-done.5), custom_call_target="tpu_custom_call" | custom-call | tf_op jit(solution)/shard_map/pallas_call | solution.py:127
  110.0 0.0 all-gather.6.cloned.1.call-done
  110.0 0.0 copy-start.1
  110.0 0.0 copy-start.6
  110.0 5.0 %shard_map.69 = bf16[4,2,64,192]{3,2,1,0:T(8,128)(2,1)} custom-call(bf16[16,4,2,2,16,512]{5,4,3,2,1,0:T(8,128)(2,1)} %bitcast.4, bf16[4,2,384,512]{3,2,1,0:T(8,128)(2,1)} %shard_map.68.dens, bf16[2,512,256]{2,1,0:T(8,128)(2,1)} %own_coeffs.1), custom_call_target="tpu_custom_call" | custom-call | tf_op jit(solution)/shard_map/pallas_call | solution.py:127
  115.1 15.5 %all_to_all.22 = bf16[4,2,64,192]{3,2,1,0:T(8,128)(2,1)S(1)} all-to-all(bf16[4,2,64,192]{3,2,1,0:T(8,128)(2,1)} %shard_map.69), channel_id=1, replica_groups=mesh['y'=4,'xh'=2,'z'=16,'xl'=2,'c'=2] {'xl','c'}, dimensions={0} | all-to-all | bytes 393216 | tf_op jit(solution)/shard_map/all_to_all | solution.py:178
  130.7 0.0 copy-done.1
  130.7 0.0 copy-done.6
  130.7 0.7 multiply_add_fusion
  (8 shorter events, 0.1 us)
Async XLA Ops:
  6.5 103.5 %all-gather.6.cloned.1.call-start = ((), (), s32[]{:S(2)}) async-start(), calls=%async_computation.4 | async-start | bytes 4456448 | tf_op jit(solution)/shard_map/all_gather | solution.py:150
  25.2 45.7 %collective-permute-start.1 = (bf16[2,512,256]{2,1,0:T(8,128)(2,1)}, bf16[2,512,256]{2,1,0:T(8,128)(2,1)S(1)}, u32[]{:S(2)}, u32[]{:S(2)}) collective-permute-start(bf16[2,512,256]{2,1,0:T(8,128)(2,1)} %own_coeffs.1), channel_id=1, source_target_pairs={{0,2},{2,0},{1,3},{3,1},{4,6},{6,4},{5,7},{7,5},{8,10},{10,8},{9,1... | collective-permute-start | bytes 1572872 | tf_op jit(solution)/shard_map/ppermute | solution.py:123
  28.3 0.8 copy-start
  56.4 16.4 %all-to-all-start.1 = ((bf16[8,16,8,192]{3,2,1,0:T(8,128)(2,1)}), bf16[8,16,8,192]{3,2,1,0:T(8,128)(2,1)S(1)}, u32[]{:S(2)}, u32[]{:S(2)}) async-start(bf16[8,16,8,192]{3,2,1,0:T(8,128)(2,1)} %broadcast_in_dim.2), calls=%async_computation.1 | async-start | bytes 1048576 | tf_op jit(solution)/shard_map/all_to_all | solution.py:139
  62.0 42.2 %collective-permute-start = (bf16[2,512,256]{2,1,0:T(8,128)(2,1)}, bf16[2,512,256]{2,1,0:T(8,128)(2,1)S(1)}, u32[]{:S(2)}, u32[]{:S(2)}) collective-permute-start(bf16[2,512,256]{2,1,0:T(8,128)(2,1)} %own_coeffs.1), channel_id=1, source_target_pairs={{0,1},{1,0},{2,3},{3,2},{4,5},{5,4},{6,7},{7,6},{8,9},{9,8},{10,11... | collective-permute-start | bytes 1572872 | tf_op jit(solution)/shard_map/ppermute | solution.py:123
  70.9 33.4 %copy-start.3 = (bf16[2,512,256]{2,1,0:T(8,128)(2,1)}, bf16[2,512,256]{2,1,0:T(8,128)(2,1)S(1)}, u32[]{:S(2)}) copy-start(bf16[2,512,256]{2,1,0:T(8,128)(2,1)S(1)} %collective-permute-done.1.refs_2_) | copy-start | bytes 1572868
  70.9 33.4 %collective-permute-start.2 = (bf16[2,512,256]{2,1,0:T(8,128)(2,1)S(1)}, bf16[2,512,256]{2,1,0:T(8,128)(2,1)S(1)}, u32[]{:S(2)}, u32[]{:S(2)}) collective-permute-start(bf16[2,512,256]{2,1,0:T(8,128)(2,1)S(1)} %collective-permute-done.1.refs_2_), channel_id=1, source_target_pairs={{0,1},{1,0},{2,3},{3,2},{4,5},{5,4},{6,7},{7,6},{8,9},{9,8},{10,11... | collective-permute-start | bytes 1572872 | tf_op jit(solution)/shard_map/ppermute | solution.py:123
  72.8 0.7 copy-start.2
  104.2 0.8 copy-start.4
  104.2 1.1 copy-start.5
  110.0 20.7 %copy-start.1 = (bf16[2,64,192]{2,1,0:T(8,128)(2,1)S(1)}, bf16[2,64,192]{2,1,0:T(8,128)(2,1)}, u32[]{:S(2)}) copy-start(bf16[2,64,192]{2,1,0:T(8,128)(2,1)} %amps.1) | copy-start | bytes 147460
  110.0 20.7 %copy-start.6 = (f32[2,64]{1,0:T(2,128)S(1)}, f32[2,64]{1,0:T(2,128)}, u32[]{:S(2)}) copy-start(f32[2,64]{1,0:T(2,128)} %param.9) | copy-start | bytes 1540
Sparse Core Ops, SparseCore 0:
  25.3 83.3 all-gather.5

commit v4 on v3

--- a/solution.py
+++ b/solution.py
@@ -5,7 +5,6 @@
 from jax.experimental.pallas import tpu as pltpu
 from jax.sharding import Mesh
 from jax.sharding import PartitionSpec as P
-
 
 KA = ("y", "xh", "z")
 COL = ("xl", "c")
@@ -25,40 +24,39 @@
         copy.wait()
 
 
-def joined(first, second, half):
-    top = lax.broadcasted_iota(jnp.int32, first.shape, 0) < 4
-    return jnp.where(top, turned(first, half[0] == 1), turned(second, half[1] == 0))
+def paired(first, second):
+    left = lax.broadcasted_iota(jnp.int32, first.shape, 1) < 64
+    return jnp.where(left, first, second)
 
 
-def turned(tile, swap):
-    other = pltpu.roll(tile, 4, 0)
-    if isinstance(swap, bool):
-        return other if swap else tile
-    return jnp.where(swap, other, tile)
+def pack_kernel(amps, out):
+    for kl in range(2):
+        out[kl * 64 : (kl + 1) * 64] = amps[kl, :, :128]
+        out[128:, kl * 64 : (kl + 1) * 64] = amps[kl, :, 128:]
 
 
-def spread_kernel(amps, out):
-    for q in range(8):
-        own = [amps[kl, 8 * q : 8 * q + 8].astype(jnp.float32) for kl in range(2)]
-        for half in range(2):
-            out[2 * q + half] = joined(own[0], own[1], (half, half)).astype(jnp.bfloat16)
+def send_kernel(partner, line, out):
+    z = lax.axis_index("z")
+    for yx in range(N_Y * N_XH):
+        for j in range(2):
+            ends = []
+            for kl in range(2):
+                wanted = partner[j, 2 * (yx * N_Z + z) + kl]
+                row, side = (wanted >> 1) & 15, wanted & 1
+                out[yx, j, kl * 64 : (kl + 1) * 64] = line[row, pl.ds(pl.multiple_of(side * 64, 64), 64)]
+                end = line[row, 128:].astype(jnp.float32)
+                ends.append(jnp.where(side == kl, end, pltpu.roll(end, 64, 1)))
+            out[yx, j, 128:] = paired(*ends).astype(jnp.bfloat16)
 
 
-def send_kernel(partner, held, out):
-    base = 2 * N_Z * lax.axis_index(PLANE)
-    for z in range(N_Z):
-        for j in range(2):
-            wanted = [partner[j, base + 2 * z + kl] for kl in range(2)]
-            tiles = [held[p >> 5, (p >> 1) & 15].astype(jnp.float32) for p in wanted]
-            out[z, j] = joined(tiles[0], tiles[1], (wanted[0] & 1, wanted[1] & 1)).astype(jnp.bfloat16)
-
-
-def keep_kernel(arrived, out):
+def keep_kernel(partner, arrived, out):
+    own = 2 * (lax.axis_index(PLANE) * N_Z + lax.axis_index("z"))
     for j in range(2):
-        for q in range(8):
-            tiles = [arrived[2 * q + half, j].astype(jnp.float32) for half in range(2)]
-            for kl in range(2):
-                out[2 * j + kl, 8 * q : 8 * q + 8] = joined(tiles[0], tiles[1], (kl, kl)).astype(jnp.bfloat16)
+        source = [partner[j, own + kl] >> 5 for kl in range(2)]
+        for kl in range(2):
+            out[j, kl * 64 : (kl + 1) * 64] = arrived[source[kl], j, kl * 64 : (kl + 1) * 64]
+        ends = [arrived[at, j, 128:].astype(jnp.float32) for at in source]
+        out[j, 128:] = paired(*ends).astype(jnp.bfloat16)
 
 
 def by_z(block):
@@ -74,8 +72,15 @@
         copy.start()
     columns = []
     for slot in range(4):
-        whole = jnp.concatenate([partners[c, slot] for c in range(N_COL)], axis=0)
-        columns.append(whole.astype(jnp.float32).T.astype(jnp.bfloat16))
+        j, kl = divmod(slot, 2)
+        own = slice(kl * 64, (kl + 1) * 64)
+        whole = [
+            jnp.concatenate(
+                [partners[c, j, own].astype(jnp.float32), partners[c, j, 128:, own].astype(jnp.float32)], axis=1
+            )
+            for c in range(N_COL)
+        ]
+        columns.append(jnp.concatenate(whole, axis=0).T.astype(jnp.bfloat16))
     vectors = [jnp.concatenate([columns[kl], columns[2 + kl]], axis=0) for kl in range(2)]
     for i in range(N_COL):
         copies[i].wait()
@@ -140,23 +145,22 @@
 
 
 def body(amps, isdf_coeffs, w_screen, energies, qsel, partner):
-    pieces = call(spread_kernel, (N_Z, 8, VEC), [VMEM], 4, amps)
-    spread = lax.all_to_all(pieces, "z", 0, 0, tiled=True)
     slabs = call(
         slab_kernel, (2, 16, 512), [SMEM, HBM], 60, qsel, w_screen, scratch=[pltpu.SemaphoreType.DMA((2,))]
     )
-    plane = lax.all_gather(lax.all_gather(slabs, "xh", axis=0, tiled=False), "y", axis=0, tiled=False)
-    plane, coeffs = lax.optimization_barrier((plane, isdf_coeffs))
+    plane = sent_to_all(slabs, PLANE)
+    plane, amps_, coeffs = lax.optimization_barrier((plane, amps, isdf_coeffs))
     rows = lax.all_gather(plane.reshape(N_Y, N_XH, 2, 16, 512), "z", axis=0, tiled=False)
 
-    held = sent_to_all(spread, PLANE)
+    packed = call(pack_kernel, (192, 128), [VMEM], 4, amps_)
+    line = lax.all_gather(packed, "z", axis=0, tiled=False)
     from_core = swapped(coeffs, "c")
     from_x = swapped(coeffs, "xl")
     from_both = swapped(from_x, "c")
 
-    send = call(send_kernel, (N_Z, 2, 8, VEC), [SMEM, VMEM], 4, partner, held)
-    arrived = lax.all_to_all(send, "z", 0, 0, tiled=True)
-    kept = call(keep_kernel, (4, 64, VEC), [VMEM], 4, arrived)
+    send = call(send_kernel, (8, 2, 192, 128), [SMEM, VMEM], 4, partner, line)
+    arrived = lax.all_to_all(send, PLANE, 0, 0, tiled=True)
+    kept = call(keep_kernel, (2, 192, 128), [SMEM, VMEM], 4, partner, arrived)
     partners = lax.all_gather(kept, COL, axis=0, tiled=False)
 
     dens = call(

time: 139 us -> 130 us (0.935)
  blocking collectives: 88.3 us -> 79.2 us
  Pallas kernels: 12.6 us -> 14.2 us
    all_to_all x2 -> x1, blocking collectives: 41.8 us -> 15.1 us  [sent_to_all(): lax.all_to_all(jnp.broadcast_to(array[None], (length, *array.shape)), axi...]
    all_gather x2 -> x1, blocking collectives: 16.6 us -> 38 us  [body(): line = lax.all_gather(packed, 'z', axis=0, tiled=False)]
    all_to_all x1, blocking collectives: 15.5 us -> 12 us  [body(): lax.all_to_all(projected, COL, 0, 0, tiled=True).astype(jnp.float32)]
    all_to_all x1, starting transfers between devices: 5.67 us -> 3.55 us  [body(): arrived = lax.all_to_all(send, PLANE, 0, 0, tiled=True)]
    pallas_call x6, Pallas kernels: 12.6 us -> 14.2 us  [call(): pl.pallas_call(kernel, out_shape=jax.ShapeDtypeStruct(shape, jnp.bfloat16...]
  transfers between devices with their start and end apart: 5 -> 5, of which waited for: 0 -> 0; matrix products, arithmetic and copies ran while one was open for 1% -> 0% of each run, Pallas kernels for 4% -> 5%
where the time goes in v4:
time: 130 us; the launch traced here: 129 us
  blocking collectives  79.2 us (61%)
  starting transfers between devices  18.3 us (14%)
  Pallas kernels  14.2 us (11%)
  between operations  13.6 us (10%)
  local copies, waits for them, and re-layouts  3.33 us (3%)
    all_gather x1, blocking collectives, body(): line = lax.all_gather(packed, 'z', axis=0, tiled=False)  38 us
    all_to_all x1, blocking collectives, sent_to_all(): lax.all_to_all(jnp.broadcast_to(array[None], (length, *array.shape)), axi...  15.1 us
    ppermute x3, starting transfers between devices, swapped(): return lax.ppermute(array, axis, [(0, 1), (1, 0)])  14.8 us
    pallas_call x6, Pallas kernels, call(): pl.pallas_call(kernel, out_shape=jax.ShapeDtypeStruct(shape, jnp.bfloat16...  14.2 us
    all_gather x1, blocking collectives, body(): partners = lax.all_gather(kept, COL, axis=0, tiled=False)  14.1 us
    all_to_all x1, blocking collectives, body(): lax.all_to_all(projected, COL, 0, 0, tiled=True).astype(jnp.float32)  12 us
    all_to_all x1, starting transfers between devices, body(): arrived = lax.all_to_all(send, PLANE, 0, 0, tiled=True)  3.55 us
  transfers between devices with their start and end apart: 5, of which 0 were waited for; matrix products, arithmetic and copies ran while one was open for 0% of the time, Pallas kernels for 5%

profile of v4, /device:TPU:1, one launch (start us, length us, event | category | flops | bytes accessed | tf_op | source)
XLA Modules:
  0.0 129.5 jit_solution(12336480327360278492)
XLA Ops:
  6.5 2.2 %shard_map.64 = bf16[2,16,512]{2,1,0:T(8,128)(2,1)} custom-call(s32[2]{0:T(128)} %qsel.1, bf16[16,16,512]{2,1,0:T(8,128)(2,1)} %w.1), custom_call_target="tpu_custom_call" | custom-call | tf_op jit(solution)/shard_map/pallas_call | solution.py:132
  8.7 0.8 broadcast_in_dim.2
  9.5 15.1 %all_to_all.15 = bf16[8,2,16,512]{3,2,1,0:T(8,128)(2,1)} all-to-all(bf16[8,2,16,512]{3,2,1,0:T(8,128)(2,1)S(1)} %broadcast_in_dim.2), channel_id=1, replica_groups=mesh['y'=4,'xh'=2,'z'=16,'xl'=2,'c'=2] {'y','xh'}, dimensions={0} | all-to-all | bytes 524288 | tf_op jit(solution)/shard_map/all_to_all | solution.py:144
  24.6 0.0 all-gather.4.cloned.1.call-update
  24.6 2.2 %collective-permute-start.1 = (bf16[2,512,256]{2,1,0:T(8,128)(2,1)}, bf16[2,512,256]{2,1,0:T(8,128)(2,1)S(1)}, u32[]{:S(2)}, u32[]{:S(2)}) collective-permute-start(bf16[2,512,256]{2,1,0:T(8,128)(2,1)} %own_coeffs.1), channel_id=1, source_target_pairs={{0,2},{2,0},{1,3},{3,1},{4,6},{6,4},{5,7},{7,5},{8,10},{10,8},{9,1... | collective-permute-start | bytes 1572872 | tf_op jit(solution)/shard_map/ppermute | solution.py:128
  26.8 0.0 copy-start
  26.8 0.8 copy-done
  27.6 0.1 shard_map.65
  27.7 38.0 %all-gather = bf16[3072,128]{1,0:T(8,128)(2,1)S(1)} all-gather(bf16[192,128]{1,0:T(8,128)(2,1)S(1)} %shard_map.65), channel_id=2, replica_groups=mesh['y'=4,'xh'=2,'z'=16,'xl'=2,'c'=2] {'z'}, dimensions={0}, use_global_device_ids=true | all-gather | bytes 835584 | tf_op jit(solution)/shard_map/all_gather | solution.py:156
  65.6 0.7 copy-done.2
  66.3 1.7 %shard_map.66 = bf16[8,2,192,128]{3,2,1,0:T(8,128)(2,1)} custom-call(s32[2,256]{1,0:T(2,128)S(1)} %copy-done.2, bf16[16,192,128]{2,1,0:T(8,128)(2,1)S(1)} %bitcast.3), custom_call_target="tpu_custom_call" | custom-call | tf_op jit(solution)/shard_map/pallas_call | solution.py:132
  68.0 3.5 %all-to-all-start.1 = ((bf16[8,2,192,128]{3,2,1,0:T(8,128)(2,1)}), bf16[8,2,192,128]{3,2,1,0:T(8,128)(2,1)S(1)}, u32[]{:S(2)}, u32[]{:S(2)}) async-start(bf16[8,2,192,128]{3,2,1,0:T(8,128)(2,1)} %shard_map.66), calls=%async_computation.1 | async-start | bytes 1572864 | tf_op jit(solution)/shard_map/all_to_all | solution.py:162
  71.6 0.0 copy-done.4
  71.6 10.7 %collective-permute-start = (bf16[2,512,256]{2,1,0:T(8,128)(2,1)S(1)}, bf16[2,512,256]{2,1,0:T(8,128)(2,1)S(1)}, u32[]{:S(2)}, u32[]{:S(2)}) collective-permute-start(bf16[2,512,256]{2,1,0:T(8,128)(2,1)S(1)} %copy-done.4), channel_id=1, source_target_pairs={{0,1},{1,0},{2,3},{3,2},{4,5},{5,4},{6,7},{7,6},{8,9},{9,8},{10,11... | collective-permute-start | bytes 1572872 | tf_op jit(solution)/shard_map/ppermute | solution.py:128
  82.3 0.0 collective-permute-done.1.refs_2_
  82.3 1.9 %collective-permute-start.2 = (bf16[2,512,256]{2,1,0:T(8,128)(2,1)S(1)}, bf16[2,512,256]{2,1,0:T(8,128)(2,1)S(1)}, u32[]{:S(2)}, u32[]{:S(2)}) collective-permute-start(bf16[2,512,256]{2,1,0:T(8,128)(2,1)S(1)} %collective-permute-done.1.refs_2_), channel_id=1, source_target_pairs={{0,1},{1,0},{2,3},{3,2},{4,5},{5,4},{6,7},{7,6},{8,9},{9,8},{10,11... | collective-permute-start | bytes 1572872 | tf_op jit(solution)/shard_map/ppermute | solution.py:128
  84.3 0.0 all-to-all-done.1.arrived
  84.3 0.6 shard_map.67
  84.9 14.1 %all-gather.1 = bf16[8,192,128]{2,1,0:T(8,128)(2,1)} all-gather(bf16[2,192,128]{2,1,0:T(8,128)(2,1)S(1)} %shard_map.67), channel_id=3, replica_groups=mesh['y'=4,'xh'=2,'z'=16,'xl'=2,'c'=2] {'xl','c'}, dimensions={0}, use_global_device_ids=true | all-gather | bytes 491520 | tf_op jit(solution)/shard_map/all_gather | solution.py:164
  99.0 0.0 collective-permute-done.refs_1_
  99.0 0.0 collective-permute-done.2.refs_3_
  99.1 0.8 copy-done.6
  99.9 0.2 copy-done.7
  100.1 4.6 %shard_map.68.dens = bf16[4,2,384,512]{3,2,1,0:T(8,128)(2,1)} custom-call(bf16[4,2,192,128]{3,2,1,0:T(8,128)(2,1)} %bitcast.4, bf16[2,512,256]{2,1,0:T(8,128)(2,1)} %own_coeffs.1, bf16[2,512,256]{2,1,0:T(8,128)(2,1)} %copy-done.6, bf16[2,512,256]{2,1,0:T(8,128)(2,1)} %copy-done.5, bf16[2,512,256]{2,1,0:T(8,128)(2,1)} %copy-done.7), custom_call_target="tpu_custom_call" | custom-call | tf_op jit(solution)/shard_map/pallas_call | solution.py:132
  104.7 0.0 copy-start.1
  104.7 0.0 copy-start.8
  104.7 0.0 all-gather.4.cloned.1.call-done.w
  104.7 5.0 %shard_map.69 = bf16[4,2,64,192]{3,2,1,0:T(8,128)(2,1)} custom-call(bf16[16,4,2,2,16,512]{5,4,3,2,1,0:T(8,128)(2,1)} %all-gather.4.cloned.1.call-done.w, bf16[4,2,384,512]{3,2,1,0:T(8,128)(2,1)} %shard_map.68.dens, bf16[2,512,256]{2,1,0:T(8,128)(2,1)} %own_coeffs.1), custom_call_target="tpu_custom_call" | custom-call | tf_op jit(solution)/shard_map/pallas_call | solution.py:132
  109.8 12.0 %all_to_all.16 = bf16[4,2,64,192]{3,2,1,0:T(8,128)(2,1)S(1)} all-to-all(bf16[4,2,64,192]{3,2,1,0:T(8,128)(2,1)} %shard_map.69), channel_id=1, replica_groups=mesh['y'=4,'xh'=2,'z'=16,'xl'=2,'c'=2] {'xl','c'}, dimensions={0} | all-to-all | bytes 393216 | tf_op jit(solution)/shard_map/all_to_all | solution.py:182
  121.8 0.0 copy-done.1
  121.9 0.0 copy-done.8
  121.9 0.7 multiply_add_fusion
  (10 shorter events, 0.1 us)
Async XLA Ops:
  6.5 65.1 %copy-start.4 = (bf16[2,512,256]{2,1,0:T(8,128)(2,1)S(1)}, bf16[2,512,256]{2,1,0:T(8,128)(2,1)}, u32[]{:S(2)}) copy-start(bf16[2,512,256]{2,1,0:T(8,128)(2,1)} %own_coeffs.1) | copy-start | bytes 1572868
  6.5 77.7 %copy-start.3 = (s32[2,256]{1,0:T(2,128)S(1)}, s32[2,256]{1,0:T(2,128)}, u32[]{:S(2)}) copy-start(s32[2,256]{1,0:T(2,128)} %partner.3) | copy-start | bytes 6148
  6.5 98.2 %all-gather.4.cloned.1.call-start = ((), (), s32[]{:S(2)}) async-start(), calls=%async_computation.3 | async-start | bytes 4456448 | tf_op jit(solution)/shard_map/all_gather | solution.py:153
  24.6 57.7 %collective-permute-start.1 = (bf16[2,512,256]{2,1,0:T(8,128)(2,1)}, bf16[2,512,256]{2,1,0:T(8,128)(2,1)S(1)}, u32[]{:S(2)}, u32[]{:S(2)}) collective-permute-start(bf16[2,512,256]{2,1,0:T(8,128)(2,1)} %own_coeffs.1), channel_id=1, source_target_pairs={{0,2},{2,0},{1,3},{3,1},{4,6},{6,4},{5,7},{7,5},{8,10},{10,8},{9,1... | collective-permute-start | bytes 1572872 | tf_op jit(solution)/shard_map/ppermute | solution.py:128
  26.8 0.8 copy-start
  65.6 0.7 copy-start.2
  68.0 16.2 %all-to-all-start.1 = ((bf16[8,2,192,128]{3,2,1,0:T(8,128)(2,1)}), bf16[8,2,192,128]{3,2,1,0:T(8,128)(2,1)S(1)}, u32[]{:S(2)}, u32[]{:S(2)}) async-start(bf16[8,2,192,128]{3,2,1,0:T(8,128)(2,1)} %shard_map.66), calls=%async_computation.1 | async-start | bytes 1572864 | tf_op jit(solution)/shard_map/all_to_all | solution.py:162
  71.6 27.4 %collective-permute-start = (bf16[2,512,256]{2,1,0:T(8,128)(2,1)S(1)}, bf16[2,512,256]{2,1,0:T(8,128)(2,1)S(1)}, u32[]{:S(2)}, u32[]{:S(2)}) collective-permute-start(bf16[2,512,256]{2,1,0:T(8,128)(2,1)S(1)} %copy-done.4), channel_id=1, source_target_pairs={{0,1},{1,0},{2,3},{3,2},{4,5},{5,4},{6,7},{7,6},{8,9},{9,8},{10,11... | collective-permute-start | bytes 1572872 | tf_op jit(solution)/shard_map/ppermute | solution.py:128
  82.3 16.7 %copy-start.5 = (bf16[2,512,256]{2,1,0:T(8,128)(2,1)}, bf16[2,512,256]{2,1,0:T(8,128)(2,1)S(1)}, u32[]{:S(2)}) copy-start(bf16[2,512,256]{2,1,0:T(8,128)(2,1)S(1)} %collective-permute-done.1.refs_2_) | copy-start | bytes 1572868
  82.3 16.7 %collective-permute-start.2 = (bf16[2,512,256]{2,1,0:T(8,128)(2,1)S(1)}, bf16[2,512,256]{2,1,0:T(8,128)(2,1)S(1)}, u32[]{:S(2)}, u32[]{:S(2)}) collective-permute-start(bf16[2,512,256]{2,1,0:T(8,128)(2,1)S(1)} %collective-permute-done.1.refs_2_), channel_id=1, source_target_pairs={{0,1},{1,0},{2,3},{3,2},{4,5},{5,4},{6,7},{7,6},{8,9},{9,8},{10,11... | collective-permute-start | bytes 1572872 | tf_op jit(solution)/shard_map/ppermute | solution.py:128
  99.0 0.8 copy-start.6
  99.0 1.0 copy-start.7
  104.7 17.2 %copy-start.1 = (bf16[2,64,192]{2,1,0:T(8,128)(2,1)S(1)}, bf16[2,64,192]{2,1,0:T(8,128)(2,1)}, u32[]{:S(2)}) copy-start(bf16[2,64,192]{2,1,0:T(8,128)(2,1)} %amps) | copy-start | bytes 147460
  104.7 17.2 %copy-start.8 = (f32[2,64]{1,0:T(2,128)S(1)}, f32[2,64]{1,0:T(2,128)}, u32[]{:S(2)}) copy-start(f32[2,64]{1,0:T(2,128)} %param.9) | copy-start | bytes 1540
Sparse Core Ops, SparseCore 0:
  24.7 75.4 all-gather.3

commit v5 on v4

--- a/solution.py
+++ b/solution.py
@@ -16,10 +16,20 @@
 HBM = pl.BlockSpec(memory_space=pltpu.HBM)
 
 
-def slab_kernel(qsel, w, out, arrived):
-    copies = [pltpu.make_async_copy(w.at[qsel[j]], out.at[j], arrived.at[j]) for j in range(2)]
+def first_kernel(qsel, w, amps, slabs, packed, own, arrived, ready):
+    fetch = pltpu.make_async_copy(amps, own, ready)
+    fetch.start()
+    copies = [
+        pltpu.make_async_copy(w.at[qsel[j]], slabs.at[to, j], arrived.at[to, j])
+        for to in range(N_Y * N_XH)
+        for j in range(2)
+    ]
     for copy in copies:
         copy.start()
+    fetch.wait()
+    for kl in range(2):
+        packed[kl * 64 : (kl + 1) * 64] = own[kl, :, :128]
+        packed[128:, kl * 64 : (kl + 1) * 64] = own[kl, :, 128:]
     for copy in copies:
         copy.wait()
 
@@ -27,12 +37,6 @@
 def paired(first, second):
     left = lax.broadcasted_iota(jnp.int32, first.shape, 1) < 64
     return jnp.where(left, first, second)
-
-
-def pack_kernel(amps, out):
-    for kl in range(2):
-        out[kl * 64 : (kl + 1) * 64] = amps[kl, :, :128]
-        out[128:, kl * 64 : (kl + 1) * 64] = amps[kl, :, 128:]
 
 
 def send_kernel(partner, line, out):
@@ -65,9 +69,8 @@
 
 
 def density_kernel(partners, *refs):
-    pieces, (out, coeffs, dens, arrived, written) = refs[:N_COL], refs[N_COL:]
+    pieces, (dens, coeffs, arrived) = refs[:N_COL], refs[N_COL:]
     copies = [pltpu.make_async_copy(pieces[i], coeffs.at[i], arrived.at[i]) for i in range(N_COL)]
-    stores = [pltpu.make_async_copy(dens.at[i], out.at[i], written.at[i]) for i in range(N_COL)]
     for copy in copies:
         copy.start()
     columns = []
@@ -90,18 +93,13 @@
             ).astype(jnp.bfloat16)
             dens[i, 0, kl * VEC : (kl + 1) * VEC, :] = part[:VEC]
             dens[i, 1, kl * VEC : (kl + 1) * VEC, :] = part[VEC:]
-        stores[i].start()
-    for store in stores:
-        store.wait()
-
-
-def screen_kernel(w, dens, own_coeffs, out, rows, held, coeffs, arrived, fetched, ready):
+
+
+def screen_kernel(w, dens, own_coeffs, out, rows, coeffs, arrived, ready):
     c = lax.axis_index(COL)
     steps = [(j, i) for j in range(2) for i in range(N_COL)]
     copies = {(j, i): pltpu.make_async_copy(w.at[:, c ^ i, :, j], rows.at[i, j], arrived.at[i, j]) for j, i in steps}
-    fetches = {(j, i): pltpu.make_async_copy(dens.at[i, j], held.at[i, j], fetched.at[i, j]) for j, i in steps}
     for step in steps:
-        fetches[step].start()
         copies[step].start()
     last = pltpu.make_async_copy(own_coeffs, coeffs, ready)
     last.start()
@@ -109,9 +107,8 @@
     for j in range(2):
         total = None
         for i in range(N_COL):
-            fetches[j, i].wait()
             copies[j, i].wait()
-            part = jnp.dot(held[i, j], rows[i, j].reshape(512, 512), preferred_element_type=jnp.float32)
+            part = jnp.dot(dens[i, j], rows[i, j].reshape(512, 512), preferred_element_type=jnp.float32)
             total = part if total is None else total + part
         screened.append(total.astype(jnp.bfloat16))
     last.wait()
@@ -121,7 +118,16 @@
         projected += jnp.dot(screened[1][own], coeffs[kl], preferred_element_type=jnp.float32)
         result = projected.T.astype(jnp.bfloat16)
         for dest in range(N_COL):
-            out[dest, kl] = result[dest * 64 : (dest + 1) * 64]
+            out[dest, kl * 64 : (kl + 1) * 64] = result[dest * 64 : (dest + 1) * 64, :128]
+            out[dest, 128:, kl * 64 : (kl + 1) * 64] = result[dest * 64 : (dest + 1) * 64, 128:]
+
+
+def last_kernel(arrived, base, out):
+    total = sum(arrived[c].astype(jnp.float32) for c in range(N_COL))
+    for kl in range(2):
+        own = slice(kl * 64, (kl + 1) * 64)
+        out[kl, :, :128] = base[kl, :, :128] + total[own]
+        out[kl, :, 128:] = base[kl, :, 128:] + total[128:, own]
 
 
 def swapped(array, axis):
@@ -131,7 +137,7 @@
 def call(kernel, shape, specs, mib, *args, scratch=(), out=VMEM):
     return pl.pallas_call(
         kernel,
-        out_shape=jax.ShapeDtypeStruct(shape, jnp.bfloat16),
+        out_shape=shape,
         in_specs=specs,
         out_specs=out,
         scratch_shapes=scratch,
@@ -139,48 +145,56 @@
     )(*args)
 
 
+def shaped(*shape, dtype=jnp.bfloat16):
+    return jax.ShapeDtypeStruct(shape, dtype)
+
+
+def in_hbm(array):
+    return pltpu.with_memory_space_constraint(array, pltpu.HBM)
+
+
 def sent_to_all(array, axis):
     length = lax.axis_size(axis)
     return lax.all_to_all(jnp.broadcast_to(array[None], (length, *array.shape)), axis, 0, 0, tiled=True)
 
 
 def body(amps, isdf_coeffs, w_screen, energies, qsel, partner):
-    slabs = call(
-        slab_kernel, (2, 16, 512), [SMEM, HBM], 60, qsel, w_screen, scratch=[pltpu.SemaphoreType.DMA((2,))]
+    slabs, packed = call(
+        first_kernel, (shaped(8, 2, 16, 512), shaped(192, 128)), [SMEM, HBM, HBM], 4,
+        qsel, in_hbm(w_screen), in_hbm(amps), out=(VMEM, VMEM),
+        scratch=[
+            pltpu.VMEM((2, 64, VEC), jnp.bfloat16), pltpu.SemaphoreType.DMA((8, 2)), pltpu.SemaphoreType.DMA,
+        ],
     )
-    plane = sent_to_all(slabs, PLANE)
-    plane, amps_, coeffs = lax.optimization_barrier((plane, amps, isdf_coeffs))
+    plane = lax.all_to_all(slabs, PLANE, 0, 0, tiled=True)
+    plane, packed, coeffs = lax.optimization_barrier((plane, packed, isdf_coeffs))
     rows = lax.all_gather(plane.reshape(N_Y, N_XH, 2, 16, 512), "z", axis=0, tiled=False)
 
-    packed = call(pack_kernel, (192, 128), [VMEM], 4, amps_)
     line = lax.all_gather(packed, "z", axis=0, tiled=False)
     from_core = swapped(coeffs, "c")
     from_x = swapped(coeffs, "xl")
     from_both = swapped(from_x, "c")
 
-    send = call(send_kernel, (8, 2, 192, 128), [SMEM, VMEM], 4, partner, line)
+    send = call(send_kernel, shaped(8, 2, 192, 128), [SMEM, VMEM], 4, partner, line)
     arrived = lax.all_to_all(send, PLANE, 0, 0, tiled=True)
-    kept = call(keep_kernel, (2, 192, 128), [SMEM, VMEM], 4, partner, arrived)
+    kept = call(keep_kernel, shaped(2, 192, 128), [SMEM, VMEM], 4, partner, arrived)
     partners = lax.all_gather(kept, COL, axis=0, tiled=False)
 
     dens = call(
-        density_kernel, (N_COL, 2, 2 * VEC, 512), [VMEM] + [HBM] * N_COL, 57,
-        partners, isdf_coeffs, from_core, from_x, from_both, out=HBM,
+        density_kernel, shaped(N_COL, 2, 2 * VEC, 512), [VMEM] + [HBM] * N_COL, 24,
+        partners, *(in_hbm(piece) for piece in (isdf_coeffs, from_core, from_x, from_both)),
+        scratch=[pltpu.VMEM((N_COL, 2, 512, 256), jnp.bfloat16), pltpu.SemaphoreType.DMA((N_COL,))],
+    )
+    projected = call(
+        screen_kernel, shaped(N_COL, 192, 128), [HBM, VMEM, HBM], 24, in_hbm(rows), dens, in_hbm(isdf_coeffs),
         scratch=[
-            pltpu.VMEM((N_COL, 2, 512, 256), jnp.bfloat16), pltpu.VMEM((N_COL, 2, 2 * VEC, 512), jnp.bfloat16),
-            pltpu.SemaphoreType.DMA((N_COL,)), pltpu.SemaphoreType.DMA((N_COL,)),
+            pltpu.VMEM((N_COL, 2, N_Z, N_XH, 16, 512), jnp.bfloat16), pltpu.VMEM((2, 512, 256), jnp.bfloat16),
+            pltpu.SemaphoreType.DMA((N_COL, 2)), pltpu.SemaphoreType.DMA,
         ],
     )
-    projected = call(
-        screen_kernel, (N_COL, 2, 64, VEC), [HBM] * 3, 60, rows, dens, isdf_coeffs,
-        scratch=[
-            pltpu.VMEM((N_COL, 2, N_Z, N_XH, 16, 512), jnp.bfloat16),
-            pltpu.VMEM((N_COL, 2, 2 * VEC, 512), jnp.bfloat16), pltpu.VMEM((2, 512, 256), jnp.bfloat16),
-            pltpu.SemaphoreType.DMA((N_COL, 2)), pltpu.SemaphoreType.DMA((N_COL, 2)), pltpu.SemaphoreType.DMA,
-        ],
-    )
-    summed = lax.all_to_all(projected, COL, 0, 0, tiled=True).astype(jnp.float32).sum(axis=0)
-    return summed + energies[:, :, None] * amps.astype(jnp.float32)
+    base = energies[:, :, None] * amps.astype(jnp.float32)
+    summed = lax.all_to_all(projected, COL, 0, 0, tiled=True)
+    return call(last_kernel, shaped(2, 64, VEC, dtype=jnp.float32), [VMEM, VMEM], 4, summed, base)
 
 
 def solution(mesh):

time: 130 us -> 128 us (0.985)
  blocking collectives: 79.2 us -> 67.7 us
  starting transfers between devices: 18.3 us -> 26.3 us
  waiting for transfers between devices: 0.05 us -> 4.05 us
  Pallas kernels: 14.2 us -> 12.7 us
    all_to_all x2 -> x1, blocking collectives: 27.1 us -> 15 us  [body(): plane = lax.all_to_all(slabs, PLANE, 0, 0, tiled=True)]
    all_to_all x0 -> x1, starting transfers between devices: none -> 8.37 us  [body(): summed = lax.all_to_all(projected, COL, 0, 0, tiled=True)]
    all_to_all x0 -> x1, waiting for transfers between devices: none -> 4 us  [body(): summed = lax.all_to_all(projected, COL, 0, 0, tiled=True)]
    pallas_call x6, Pallas kernels: 14.2 us -> 12.7 us  [call(): pl.pallas_call(kernel, out_shape=shape, in_specs=specs, out_specs=out, sc...]
  transfers between devices with their start and end apart: 5 -> 6, of which waited for: 0 -> 1; matrix products, arithmetic and copies ran while one was open for 0% -> 0% of each run, Pallas kernels for 5% -> 4%
where the time goes in v5:
time: 128 us; the launch traced here: 127 us
  blocking collectives  67.7 us (53%)
  starting transfers between devices  26.3 us (21%)
  between operations  13.5 us (11%)
  Pallas kernels  12.7 us (10%)
  waiting for transfers between devices  4.05 us (3%)
  local copies, waits for them, and re-layouts  2.96 us (2%)
    all_gather x1, blocking collectives, body(): line = lax.all_gather(packed, 'z', axis=0, tiled=False)  39 us
    all_to_all x1, blocking collectives, body(): plane = lax.all_to_all(slabs, PLANE, 0, 0, tiled=True)  15 us
    ppermute x3, starting transfers between devices, swapped(): return lax.ppermute(array, axis, [(0, 1), (1, 0)])  14.4 us
    all_gather x1, blocking collectives, body(): partners = lax.all_gather(kept, COL, axis=0, tiled=False)  13.6 us
    pallas_call x6, Pallas kernels, call(): pl.pallas_call(kernel, out_shape=shape, in_specs=specs, out_specs=out, sc...  12.7 us
    all_to_all x1, starting transfers between devices, body(): summed = lax.all_to_all(projected, COL, 0, 0, tiled=True)  8.37 us
    all_to_all x1, waiting for transfers between devices, body(): summed = lax.all_to_all(projected, COL, 0, 0, tiled=True)  4 us
    all_to_all x1, starting transfers between devices, body(): arrived = lax.all_to_all(send, PLANE, 0, 0, tiled=True)  3.55 us
  transfers between devices with their start and end apart: 6, of which 1 were waited for; matrix products, arithmetic and copies ran while one was open for 0% of the time, Pallas kernels for 4%

profile of v5, /device:TPU:1, one launch (start us, length us, event | category | flops | bytes accessed | tf_op | source)
XLA Modules:
  0.0 127.3 jit_solution(11219589903380157368)
XLA Ops:
  6.5 0.0 all-gather.4.cloned.1.call-start
  6.5 0.7 copy-done.2
  7.2 2.0 %shard_map.64 = (bf16[8,2,16,512]{3,2,1,0:T(8,128)(2,1)S(1)}, bf16[192,128]{1,0:T(8,128)(2,1)S(1)}) custom-call(s32[2]{0:T(128)S(1)} %copy-done.2, bf16[16,16,512]{2,1,0:T(8,128)(2,1)} %w.1, bf16[2,64,192]{2,1,0:T(8,128)(2,1)} %amps.1), custom_call_target="tpu_custom_call" | custom-call | tf_op jit(solution)/shard_map/pallas_call | solution.py:138
  9.2 15.0 %all_to_all.15 = bf16[8,2,16,512]{3,2,1,0:T(8,128)(2,1)} all-to-all(bf16[8,2,16,512]{3,2,1,0:T(8,128)(2,1)S(1)} %get-tuple-element.10), channel_id=1, replica_groups=mesh['y'=4,'xh'=2,'z'=16,'xl'=2,'c'=2] {'y','xh'}, dimensions={0} | all-to-all | bytes 524288 | tf_op jit(solution)/shard_map/all_to_all | solution.py:169
  24.3 0.0 all-gather.4.cloned.1.call-update
  24.3 2.2 %collective-permute-start.1 = (bf16[2,512,256]{2,1,0:T(8,128)(2,1)}, bf16[2,512,256]{2,1,0:T(8,128)(2,1)S(1)}, u32[]{:S(2)}, u32[]{:S(2)}) collective-permute-start(bf16[2,512,256]{2,1,0:T(8,128)(2,1)} %own_coeffs.1), channel_id=1, source_target_pairs={{0,2},{2,0},{1,3},{3,1},{4,6},{6,4},{5,7},{7,5},{8,10},{10,8},{9,1... | collective-permute-start | bytes 1572872 | tf_op jit(solution)/shard_map/ppermute | solution.py:134
  26.5 39.0 %all-gather = bf16[3072,128]{1,0:T(8,128)(2,1)S(1)} all-gather(bf16[192,128]{1,0:T(8,128)(2,1)S(1)} %get-tuple-element.13), channel_id=2, replica_groups=mesh['y'=4,'xh'=2,'z'=16,'xl'=2,'c'=2] {'z'}, dimensions={0}, use_global_device_ids=true | all-gather | bytes 835584 | tf_op jit(solution)/shard_map/all_gather | solution.py:173
  65.6 0.7 copy-done
  66.2 1.8 %shard_map.65 = bf16[8,2,192,128]{3,2,1,0:T(8,128)(2,1)} custom-call(s32[2,256]{1,0:T(2,128)S(1)} %copy-done, bf16[16,192,128]{2,1,0:T(8,128)(2,1)S(1)} %bitcast.3), custom_call_target="tpu_custom_call" | custom-call | tf_op jit(solution)/shard_map/pallas_call | solution.py:138
  68.0 3.5 %all-to-all-start.1 = ((bf16[8,2,192,128]{3,2,1,0:T(8,128)(2,1)}), bf16[8,2,192,128]{3,2,1,0:T(8,128)(2,1)S(1)}, u32[]{:S(2)}, u32[]{:S(2)}) async-start(bf16[8,2,192,128]{3,2,1,0:T(8,128)(2,1)} %shard_map.65), calls=%async_computation.1 | async-start | bytes 1572864 | tf_op jit(solution)/shard_map/all_to_all | solution.py:179
  71.5 0.0 copy-done.3
  71.6 10.3 %collective-permute-start = (bf16[2,512,256]{2,1,0:T(8,128)(2,1)S(1)}, bf16[2,512,256]{2,1,0:T(8,128)(2,1)S(1)}, u32[]{:S(2)}, u32[]{:S(2)}) collective-permute-start(bf16[2,512,256]{2,1,0:T(8,128)(2,1)S(1)} %copy-done.3), channel_id=1, source_target_pairs={{0,1},{1,0},{2,3},{3,2},{4,5},{5,4},{6,7},{7,6},{8,9},{9,8},{10,11... | collective-permute-start | bytes 1572872 | tf_op jit(solution)/shard_map/ppermute | solution.py:134
  81.8 0.0 collective-permute-done.1.refs_2_
  81.8 0.0 copy-start.4
  81.8 1.9 %collective-permute-start.2 = (bf16[2,512,256]{2,1,0:T(8,128)(2,1)S(1)}, bf16[2,512,256]{2,1,0:T(8,128)(2,1)S(1)}, u32[]{:S(2)}, u32[]{:S(2)}) collective-permute-start(bf16[2,512,256]{2,1,0:T(8,128)(2,1)S(1)} %collective-permute-done.1.refs_2_), channel_id=1, source_target_pairs={{0,1},{1,0},{2,3},{3,2},{4,5},{5,4},{6,7},{7,6},{8,9},{9,8},{10,11... | collective-permute-start | bytes 1572872 | tf_op jit(solution)/shard_map/ppermute | solution.py:134
  83.8 0.0 all-to-all-done.1.arrived
  83.8 0.0 copy-done.1
  83.8 0.6 shard_map.66
  84.4 13.6 %all-gather.1 = bf16[8,192,128]{2,1,0:T(8,128)(2,1)S(1)} all-gather(bf16[2,192,128]{2,1,0:T(8,128)(2,1)S(1)} %shard_map.66), channel_id=3, replica_groups=mesh['y'=4,'xh'=2,'z'=16,'xl'=2,'c'=2] {'xl','c'}, dimensions={0}, use_global_device_ids=true | all-gather | bytes 491520 | tf_op jit(solution)/shard_map/all_gather | solution.py:181
  98.0 0.0 collective-permute-done.refs_1_
  98.0 0.0 collective-permute-done.2.refs_3_
  98.0 0.8 copy-done.5
  98.8 0.8 copy-done.6
  99.6 2.9 %shard_map.67.dens = bf16[4,2,384,512]{3,2,1,0:T(8,128)(2,1)S(1)} custom-call(bf16[4,2,192,128]{3,2,1,0:T(8,128)(2,1)S(1)} %bitcast.4, bf16[2,512,256]{2,1,0:T(8,128)(2,1)} %own_coeffs.1, bf16[2,512,256]{2,1,0:T(8,128)(2,1)} %copy-done.5, bf16[2,512,256]{2,1,0:T(8,128)(2,1)} %copy-done.4, bf16[2,512,256]{2,1,0:T(8,128)(2,1)} %copy-done.6), custom_call_target="tpu_custom_call" | custom-call | tf_op jit(solution)/shard_map/pallas_call | solution.py:138
  102.5 0.0 copy-start.7
  102.5 0.0 copy-start.8
  102.5 0.0 all-gather.4.cloned.1.call-done.w
  102.5 4.7 %shard_map.68 = bf16[4,192,128]{2,1,0:T(8,128)(2,1)} custom-call(bf16[16,4,2,2,16,512]{5,4,3,2,1,0:T(8,128)(2,1)} %all-gather.4.cloned.1.call-done.w, bf16[4,2,384,512]{3,2,1,0:T(8,128)(2,1)S(1)} %shard_map.67.dens, bf16[2,512,256]{2,1,0:T(8,128)(2,1)} %own_coeffs.1), custom_call_target="tpu_custom_call" | custom-call | tf_op jit(solution)/shard_map/pallas_call | solution.py:138
  107.3 8.4 %all-to-all-start.2 = ((bf16[4,192,128]{2,1,0:T(8,128)(2,1)}), bf16[4,192,128]{2,1,0:T(8,128)(2,1)S(1)}, u32[]{:S(2)}, u32[]{:S(2)}) async-start(bf16[4,192,128]{2,1,0:T(8,128)(2,1)} %shard_map.68), calls=%async_computation.2 | async-start | bytes 393216 | tf_op jit(solution)/shard_map/all_to_all | solution.py:196
  115.7 0.1 convert_multiply_fusion.base
  115.7 4.0 %all-to-all-done.2.arrived = bf16[4,192,128]{2,1,0:T(8,128)(2,1)S(1)} async-done(((bf16[4,192,128]{2,1,0:T(8,128)(2,1)}), bf16[4,192,128]{2,1,0:T(8,128)(2,1)S(1)}, u32[]{:S(2)}, u32[]{:S(2)}) %all-to-all-start.2) | async-done | bytes 196640 | tf_op jit(solution)/shard_map/all_to_all | solution.py:196
  119.7 0.7 shard_map.69
  (9 shorter events, 0.0 us)
Async XLA Ops:
  6.5 77.2 %copy-start.1 = (s32[2,256]{1,0:T(2,128)S(1)}, s32[2,256]{1,0:T(2,128)}, u32[]{:S(2)}) copy-start(s32[2,256]{1,0:T(2,128)} %partner.3) | copy-start | bytes 6148
  6.5 96.0 %all-gather.4.cloned.1.call-start = ((), (), s32[]{:S(2)}) async-start(), calls=%async_computation.3 | async-start | bytes 4456448 | tf_op jit(solution)/shard_map/all_gather | solution.py:171
  6.5 0.7 copy-start.2
  7.2 64.3 %copy-start.3 = (bf16[2,512,256]{2,1,0:T(8,128)(2,1)S(1)}, bf16[2,512,256]{2,1,0:T(8,128)(2,1)}, u32[]{:S(2)}) copy-start(bf16[2,512,256]{2,1,0:T(8,128)(2,1)} %own_coeffs.1) | copy-start | bytes 1572868
  24.3 57.5 %collective-permute-start.1 = (bf16[2,512,256]{2,1,0:T(8,128)(2,1)}, bf16[2,512,256]{2,1,0:T(8,128)(2,1)S(1)}, u32[]{:S(2)}, u32[]{:S(2)}) collective-permute-start(bf16[2,512,256]{2,1,0:T(8,128)(2,1)} %own_coeffs.1), channel_id=1, source_target_pairs={{0,2},{2,0},{1,3},{3,1},{4,6},{6,4},{5,7},{7,5},{8,10},{10,8},{9,1... | collective-permute-start | bytes 1572872 | tf_op jit(solution)/shard_map/ppermute | solution.py:134
  65.6 0.7 copy-start
  68.0 15.8 %all-to-all-start.1 = ((bf16[8,2,192,128]{3,2,1,0:T(8,128)(2,1)}), bf16[8,2,192,128]{3,2,1,0:T(8,128)(2,1)S(1)}, u32[]{:S(2)}, u32[]{:S(2)}) async-start(bf16[8,2,192,128]{3,2,1,0:T(8,128)(2,1)} %shard_map.65), calls=%async_computation.1 | async-start | bytes 1572864 | tf_op jit(solution)/shard_map/all_to_all | solution.py:179
  71.6 26.5 %collective-permute-start = (bf16[2,512,256]{2,1,0:T(8,128)(2,1)S(1)}, bf16[2,512,256]{2,1,0:T(8,128)(2,1)S(1)}, u32[]{:S(2)}, u32[]{:S(2)}) collective-permute-start(bf16[2,512,256]{2,1,0:T(8,128)(2,1)S(1)} %copy-done.3), channel_id=1, source_target_pairs={{0,1},{1,0},{2,3},{3,2},{4,5},{5,4},{6,7},{7,6},{8,9},{9,8},{10,11... | collective-permute-start | bytes 1572872 | tf_op jit(solution)/shard_map/ppermute | solution.py:134
  81.8 16.2 %copy-start.4 = (bf16[2,512,256]{2,1,0:T(8,128)(2,1)}, bf16[2,512,256]{2,1,0:T(8,128)(2,1)S(1)}, u32[]{:S(2)}) copy-start(bf16[2,512,256]{2,1,0:T(8,128)(2,1)S(1)} %collective-permute-done.1.refs_2_) | copy-start | bytes 1572868
  81.8 16.2 %collective-permute-start.2 = (bf16[2,512,256]{2,1,0:T(8,128)(2,1)S(1)}, bf16[2,512,256]{2,1,0:T(8,128)(2,1)S(1)}, u32[]{:S(2)}, u32[]{:S(2)}) collective-permute-start(bf16[2,512,256]{2,1,0:T(8,128)(2,1)S(1)} %collective-permute-done.1.refs_2_), channel_id=1, source_target_pairs={{0,1},{1,0},{2,3},{3,2},{4,5},{5,4},{6,7},{7,6},{8,9},{9,8},{10,11... | collective-permute-start | bytes 1572872 | tf_op jit(solution)/shard_map/ppermute | solution.py:134
  98.0 0.8 copy-start.5
  98.8 0.8 copy-start.6
  102.5 13.2 %copy-start.7 = (bf16[2,64,192]{2,1,0:T(8,128)(2,1)S(1)}, bf16[2,64,192]{2,1,0:T(8,128)(2,1)}, u32[]{:S(2)}) copy-start(bf16[2,64,192]{2,1,0:T(8,128)(2,1)} %amps.1) | copy-start | bytes 147460
  102.5 13.2 %copy-start.8 = (f32[2,64]{1,0:T(2,128)S(1)}, f32[2,64]{1,0:T(2,128)}, u32[]{:S(2)}) copy-start(f32[2,64]{1,0:T(2,128)} %param.9) | copy-start | bytes 1540
  107.3 12.5 %all-to-all-start.2 = ((bf16[4,192,128]{2,1,0:T(8,128)(2,1)}), bf16[4,192,128]{2,1,0:T(8,128)(2,1)S(1)}, u32[]{:S(2)}, u32[]{:S(2)}) async-start(bf16[4,192,128]{2,1,0:T(8,128)(2,1)} %shard_map.68), calls=%async_computation.2 | async-start | bytes 393216 | tf_op jit(solution)/shard_map/all_to_all | solution.py:196
Sparse Core Ops, SparseCore 0:
  24.4 75.0 all-gather.3

commit v6 on v5

--- a/solution.py
+++ b/solution.py
@@ -161,7 +161,7 @@
 def body(amps, isdf_coeffs, w_screen, energies, qsel, partner):
     slabs, packed = call(
         first_kernel, (shaped(8, 2, 16, 512), shaped(192, 128)), [SMEM, HBM, HBM], 4,
-        qsel, in_hbm(w_screen), in_hbm(amps), out=(VMEM, VMEM),
+        in_hbm(qsel), in_hbm(w_screen), in_hbm(amps), out=(VMEM, VMEM),
         scratch=[
             pltpu.VMEM((2, 64, VEC), jnp.bfloat16), pltpu.SemaphoreType.DMA((8, 2)), pltpu.SemaphoreType.DMA,
         ],
@@ -175,9 +175,9 @@
     from_x = swapped(coeffs, "xl")
     from_both = swapped(from_x, "c")
 
-    send = call(send_kernel, shaped(8, 2, 192, 128), [SMEM, VMEM], 4, partner, line)
+    send = call(send_kernel, pltpu.VMEM((8, 2, 192, 128), jnp.bfloat16), [SMEM, VMEM], 4, in_hbm(partner), line)
     arrived = lax.all_to_all(send, PLANE, 0, 0, tiled=True)
-    kept = call(keep_kernel, shaped(2, 192, 128), [SMEM, VMEM], 4, partner, arrived)
+    kept = call(keep_kernel, shaped(2, 192, 128), [SMEM, VMEM], 4, in_hbm(partner), arrived)
     partners = lax.all_gather(kept, COL, axis=0, tiled=False)
 
     dens = call(
@@ -185,14 +185,15 @@
         partners, *(in_hbm(piece) for piece in (isdf_coeffs, from_core, from_x, from_both)),
         scratch=[pltpu.VMEM((N_COL, 2, 512, 256), jnp.bfloat16), pltpu.SemaphoreType.DMA((N_COL,))],
     )
+    base = energies[:, :, None] * amps.astype(jnp.float32)
+    dens, base = lax.optimization_barrier((dens, base))
     projected = call(
-        screen_kernel, shaped(N_COL, 192, 128), [HBM, VMEM, HBM], 24, in_hbm(rows), dens, in_hbm(isdf_coeffs),
+        screen_kernel, pltpu.VMEM((N_COL, 192, 128), jnp.bfloat16), [HBM, VMEM, HBM], 24, in_hbm(rows), dens, in_hbm(isdf_coeffs),
         scratch=[
             pltpu.VMEM((N_COL, 2, N_Z, N_XH, 16, 512), jnp.bfloat16), pltpu.VMEM((2, 512, 256), jnp.bfloat16),
             pltpu.SemaphoreType.DMA((N_COL, 2)), pltpu.SemaphoreType.DMA,
         ],
     )
-    base = energies[:, :, None] * amps.astype(jnp.float32)
     summed = lax.all_to_all(projected, COL, 0, 0, tiled=True)
     return call(last_kernel, shaped(2, 64, VEC, dtype=jnp.float32), [VMEM, VMEM], 4, summed, base)
 

time: 128 us -> 126 us (0.984)
  blocking collectives: 67.7 us -> 80.2 us
  starting transfers between devices: 26.3 us -> 17.9 us
  waiting for transfers between devices: 4.05 us -> 0.05 us
  local copies, waits for them, and re-layouts: 2.96 us -> 1.62 us
    all_to_all x0 -> x1, blocking collectives: none -> 12.6 us  [body(): summed = lax.all_to_all(projected, COL, 0, 0, tiled=True)]
    all_to_all x1 -> x0, starting transfers between devices: 8.37 us -> none  [body(): summed = lax.all_to_all(projected, COL, 0, 0, tiled=True)]
    all_to_all x1 -> x0, waiting for transfers between devices: 4 us -> none  [body(): summed = lax.all_to_all(projected, COL, 0, 0, tiled=True)]
    unnamed x18 -> x12, local copies, waits for them, and re-layouts: 2.96 us -> 1.62 us
  transfers between devices with their start and end apart: 6 -> 5, of which waited for: 1 -> 0; matrix products, arithmetic and copies ran while one was open for 0% -> 0% of each run, Pallas kernels for 4% -> 4%
where the time goes in v6:
time: 126 us
  blocking collectives  80.2 us (64%)
  starting transfers between devices  17.9 us (14%)
  between operations  13.5 us (11%)
  Pallas kernels  12.5 us (10%)
  local copies, waits for them, and re-layouts  1.62 us (1%)
    all_gather x1, blocking collectives, body(): line = lax.all_gather(packed, 'z', axis=0, tiled=False)  39 us
    all_to_all x1, blocking collectives, body(): plane = lax.all_to_all(slabs, PLANE, 0, 0, tiled=True)  15.1 us
    ppermute x3, starting transfers between devices, swapped(): return lax.ppermute(array, axis, [(0, 1), (1, 0)])  14.4 us
    all_gather x1, blocking collectives, body(): partners = lax.all_gather(kept, COL, axis=0, tiled=False)  13.5 us
    all_to_all x1, blocking collectives, body(): summed = lax.all_to_all(projected, COL, 0, 0, tiled=True)  12.6 us
    pallas_call x6, Pallas kernels, call(): pl.pallas_call(kernel, out_shape=shape, in_specs=specs, out_specs=out, sc...  12.5 us
    all_to_all x1, starting transfers between devices, body(): arrived = lax.all_to_all(send, PLANE, 0, 0, tiled=True)  3.55 us
  transfers between devices with their start and end apart: 5, of which 0 were waited for; matrix products, arithmetic and copies ran while one was open for 0% of the time, Pallas kernels for 4%

profile of v6, /device:TPU:1, one launch (start us, length us, event | category | flops | bytes accessed | tf_op | source)
XLA Modules:
  0.0 125.9 jit_solution(16467140885816859405)
XLA Ops:
  6.5 0.0 copy-start.4
  6.5 0.0 copy-start
  6.5 0.0 copy-start.5
  6.5 0.0 all-gather.4.cloned.1.call-start
  6.5 2.3 %shard_map.64 = (bf16[8,2,16,512]{3,2,1,0:T(8,128)(2,1)S(1)}, bf16[192,128]{1,0:T(8,128)(2,1)S(1)}) custom-call(s32[2]{0:T(128)} %qsel.1, bf16[16,16,512]{2,1,0:T(8,128)(2,1)} %w.1, bf16[2,64,192]{2,1,0:T(8,128)(2,1)} %amps.1), custom_call_target="tpu_custom_call" | custom-call | tf_op jit(solution)/shard_map/pallas_call | solution.py:138
  8.8 15.1 %all_to_all.15 = bf16[8,2,16,512]{3,2,1,0:T(8,128)(2,1)} all-to-all(bf16[8,2,16,512]{3,2,1,0:T(8,128)(2,1)S(1)} %get-tuple-element.12), channel_id=1, replica_groups=mesh['y'=4,'xh'=2,'z'=16,'xl'=2,'c'=2] {'y','xh'}, dimensions={0} | all-to-all | bytes 524288 | tf_op jit(solution)/shard_map/all_to_all | solution.py:169
  23.9 0.0 all-gather.4.cloned.1.call-update
  23.9 2.2 %collective-permute-start.1 = (bf16[2,512,256]{2,1,0:T(8,128)(2,1)}, bf16[2,512,256]{2,1,0:T(8,128)(2,1)S(1)}, u32[]{:S(2)}, u32[]{:S(2)}) collective-permute-start(bf16[2,512,256]{2,1,0:T(8,128)(2,1)} %own_coeffs.1), channel_id=1, source_target_pairs={{0,2},{2,0},{1,3},{3,1},{4,6},{6,4},{5,7},{7,5},{8,10},{10,8},{9,1... | collective-permute-start | bytes 1572872 | tf_op jit(solution)/shard_map/ppermute | solution.py:134
  26.1 39.0 %all-gather = bf16[3072,128]{1,0:T(8,128)(2,1)S(1)} all-gather(bf16[192,128]{1,0:T(8,128)(2,1)S(1)} %get-tuple-element.15), channel_id=2, replica_groups=mesh['y'=4,'xh'=2,'z'=16,'xl'=2,'c'=2] {'z'}, dimensions={0}, use_global_device_ids=true | all-gather | bytes 835584 | tf_op jit(solution)/shard_map/all_gather | solution.py:173
  65.1 1.9 %shard_map.65 = bf16[8,2,192,128]{3,2,1,0:T(8,128)(2,1)} custom-call(s32[2,256]{1,0:T(2,128)} %partner.3, bf16[16,192,128]{2,1,0:T(8,128)(2,1)S(1)} %bitcast.3), custom_call_target="tpu_custom_call" | custom-call | tf_op jit(solution)/shard_map/pallas_call | solution.py:138
  67.0 3.5 %all-to-all-start.1 = ((bf16[8,2,192,128]{3,2,1,0:T(8,128)(2,1)}), bf16[8,2,192,128]{3,2,1,0:T(8,128)(2,1)S(1)}, u32[]{:S(2)}, u32[]{:S(2)}) async-start(bf16[8,2,192,128]{3,2,1,0:T(8,128)(2,1)} %shard_map.65), calls=%async_computation.1 | async-start | bytes 1572864 | tf_op jit(solution)/shard_map/all_to_all | solution.py:179
  70.5 0.0 copy-done
  70.6 10.3 %collective-permute-start = (bf16[2,512,256]{2,1,0:T(8,128)(2,1)S(1)}, bf16[2,512,256]{2,1,0:T(8,128)(2,1)S(1)}, u32[]{:S(2)}, u32[]{:S(2)}) collective-permute-start(bf16[2,512,256]{2,1,0:T(8,128)(2,1)S(1)} %copy-done), channel_id=1, source_target_pairs={{0,1},{1,0},{2,3},{3,2},{4,5},{5,4},{6,7},{7,6},{8,9},{9,8},{10,11... | collective-permute-start | bytes 1572872 | tf_op jit(solution)/shard_map/ppermute | solution.py:134
  80.8 0.0 collective-permute-done.1.refs_2_
  80.8 0.0 copy-start.1
  80.8 1.9 %collective-permute-start.2 = (bf16[2,512,256]{2,1,0:T(8,128)(2,1)S(1)}, bf16[2,512,256]{2,1,0:T(8,128)(2,1)S(1)}, u32[]{:S(2)}, u32[]{:S(2)}) collective-permute-start(bf16[2,512,256]{2,1,0:T(8,128)(2,1)S(1)} %collective-permute-done.1.refs_2_), channel_id=1, source_target_pairs={{0,1},{1,0},{2,3},{3,2},{4,5},{5,4},{6,7},{7,6},{8,9},{9,8},{10,11... | collective-permute-start | bytes 1572872 | tf_op jit(solution)/shard_map/ppermute | solution.py:134
  82.8 0.0 copy-done.4
  82.8 0.0 copy-done.5
  82.8 0.1 convert_multiply_fusion.base
  82.9 0.0 all-to-all-done.1.arrived
  82.9 0.7 shard_map.66
  83.6 13.5 %all-gather.1 = bf16[8,192,128]{2,1,0:T(8,128)(2,1)S(1)} all-gather(bf16[2,192,128]{2,1,0:T(8,128)(2,1)S(1)} %shard_map.66), channel_id=3, replica_groups=mesh['y'=4,'xh'=2,'z'=16,'xl'=2,'c'=2] {'xl','c'}, dimensions={0}, use_global_device_ids=true | all-gather | bytes 491520 | tf_op jit(solution)/shard_map/all_gather | solution.py:181
  97.1 0.0 collective-permute-done.refs_1_
  97.1 0.0 collective-permute-done.2.refs_3_
  97.1 0.0 copy-done.1
  97.2 0.8 copy-done.2
  98.0 0.8 copy-done.3
  98.8 2.9 %shard_map.67.dens = bf16[4,2,384,512]{3,2,1,0:T(8,128)(2,1)S(1)} custom-call(bf16[4,2,192,128]{3,2,1,0:T(8,128)(2,1)S(1)} %bitcast.4, bf16[2,512,256]{2,1,0:T(8,128)(2,1)} %own_coeffs.1, bf16[2,512,256]{2,1,0:T(8,128)(2,1)} %copy-done.2, bf16[2,512,256]{2,1,0:T(8,128)(2,1)} %copy-done.1, bf16[2,512,256]{2,1,0:T(8,128)(2,1)} %copy-done.3), custom_call_target="tpu_custom_call" | custom-call | tf_op jit(solution)/shard_map/pallas_call | solution.py:138
  101.6 0.0 all-gather.4.cloned.1.call-done.w
  101.7 4.1 %shard_map.68 = bf16[4,192,128]{2,1,0:T(8,128)(2,1)S(1)} custom-call(bf16[16,4,2,2,16,512]{5,4,3,2,1,0:T(8,128)(2,1)} %all-gather.4.cloned.1.call-done.w, bf16[4,2,384,512]{3,2,1,0:T(8,128)(2,1)S(1)} %shard_map.67.dens, bf16[2,512,256]{2,1,0:T(8,128)(2,1)} %own_coeffs.1), custom_call_target="tpu_custom_call" | custom-call | tf_op jit(solution)/shard_map/pallas_call | solution.py:138
  105.7 12.6 %all_to_all.16.arrived = bf16[4,192,128]{2,1,0:T(8,128)(2,1)S(1)} all-to-all(bf16[4,192,128]{2,1,0:T(8,128)(2,1)S(1)} %shard_map.68), channel_id=1, replica_groups=mesh['y'=4,'xh'=2,'z'=16,'xl'=2,'c'=2] {'xl','c'}, dimensions={0} | all-to-all | bytes 393216 | tf_op jit(solution)/shard_map/all_to_all | solution.py:197
  118.3 0.7 shard_map.69
  (2 shorter events, 0.0 us)
Async XLA Ops:
  6.5 76.2 %copy-start.4 = (bf16[2,64,192]{2,1,0:T(8,128)(2,1)S(1)}, bf16[2,64,192]{2,1,0:T(8,128)(2,1)}, u32[]{:S(2)}) copy-start(bf16[2,64,192]{2,1,0:T(8,128)(2,1)} %amps.1) | copy-start | bytes 147460
  6.5 64.0 %copy-start = (bf16[2,512,256]{2,1,0:T(8,128)(2,1)S(1)}, bf16[2,512,256]{2,1,0:T(8,128)(2,1)}, u32[]{:S(2)}) copy-start(bf16[2,512,256]{2,1,0:T(8,128)(2,1)} %own_coeffs.1) | copy-start | bytes 1572868
  6.5 76.2 %copy-start.5 = (f32[2,64]{1,0:T(2,128)S(1)}, f32[2,64]{1,0:T(2,128)}, u32[]{:S(2)}) copy-start(f32[2,64]{1,0:T(2,128)} %param.9) | copy-start | bytes 1540
  6.5 95.1 %all-gather.4.cloned.1.call-start = ((), (), s32[]{:S(2)}) async-start(), calls=%async_computation.3 | async-start | bytes 4456448 | tf_op jit(solution)/shard_map/all_gather | solution.py:171
  23.9 56.9 %collective-permute-start.1 = (bf16[2,512,256]{2,1,0:T(8,128)(2,1)}, bf16[2,512,256]{2,1,0:T(8,128)(2,1)S(1)}, u32[]{:S(2)}, u32[]{:S(2)}) collective-permute-start(bf16[2,512,256]{2,1,0:T(8,128)(2,1)} %own_coeffs.1), channel_id=1, source_target_pairs={{0,2},{2,0},{1,3},{3,1},{4,6},{6,4},{5,7},{7,5},{8,10},{10,8},{9,1... | collective-permute-start | bytes 1572872 | tf_op jit(solution)/shard_map/ppermute | solution.py:134
  67.0 15.9 %all-to-all-start.1 = ((bf16[8,2,192,128]{3,2,1,0:T(8,128)(2,1)}), bf16[8,2,192,128]{3,2,1,0:T(8,128)(2,1)S(1)}, u32[]{:S(2)}, u32[]{:S(2)}) async-start(bf16[8,2,192,128]{3,2,1,0:T(8,128)(2,1)} %shard_map.65), calls=%async_computation.1 | async-start | bytes 1572864 | tf_op jit(solution)/shard_map/all_to_all | solution.py:179
  70.6 26.6 %collective-permute-start = (bf16[2,512,256]{2,1,0:T(8,128)(2,1)S(1)}, bf16[2,512,256]{2,1,0:T(8,128)(2,1)S(1)}, u32[]{:S(2)}, u32[]{:S(2)}) collective-permute-start(bf16[2,512,256]{2,1,0:T(8,128)(2,1)S(1)} %copy-done), channel_id=1, source_target_pairs={{0,1},{1,0},{2,3},{3,2},{4,5},{5,4},{6,7},{7,6},{8,9},{9,8},{10,11... | collective-permute-start | bytes 1572872 | tf_op jit(solution)/shard_map/ppermute | solution.py:134
  80.8 16.3 %copy-start.1 = (bf16[2,512,256]{2,1,0:T(8,128)(2,1)}, bf16[2,512,256]{2,1,0:T(8,128)(2,1)S(1)}, u32[]{:S(2)}) copy-start(bf16[2,512,256]{2,1,0:T(8,128)(2,1)S(1)} %collective-permute-done.1.refs_2_) | copy-start | bytes 1572868
  80.8 16.3 %collective-permute-start.2 = (bf16[2,512,256]{2,1,0:T(8,128)(2,1)S(1)}, bf16[2,512,256]{2,1,0:T(8,128)(2,1)S(1)}, u32[]{:S(2)}, u32[]{:S(2)}) collective-permute-start(bf16[2,512,256]{2,1,0:T(8,128)(2,1)S(1)} %collective-permute-done.1.refs_2_), channel_id=1, source_target_pairs={{0,1},{1,0},{2,3},{3,2},{4,5},{5,4},{6,7},{7,6},{8,9},{9,8},{10,11... | collective-permute-start | bytes 1572872 | tf_op jit(solution)/shard_map/ppermute | solution.py:134
  97.1 0.8 copy-start.2
  98.0 0.8 copy-start.3
Sparse Core Ops, SparseCore 0:
  24.0 74.6 all-gather.3

commit v7 on v6

--- a/solution.py
+++ b/solution.py
@@ -167,10 +167,11 @@
         ],
     )
     plane = lax.all_to_all(slabs, PLANE, 0, 0, tiled=True)
-    plane, packed, coeffs = lax.optimization_barrier((plane, packed, isdf_coeffs))
+    plane, packed = lax.optimization_barrier((plane, packed))
     rows = lax.all_gather(plane.reshape(N_Y, N_XH, 2, 16, 512), "z", axis=0, tiled=False)
 
     line = lax.all_gather(packed, "z", axis=0, tiled=False)
+    line, coeffs = lax.optimization_barrier((line, isdf_coeffs))
     from_core = swapped(coeffs, "c")
     from_x = swapped(coeffs, "xl")
     from_both = swapped(from_x, "c")

time: 126 us -> 126 us (level)
  blocking collectives: 80.2 us -> 76.9 us
  starting transfers between devices: 17.9 us -> 20.6 us
    ppermute x3, starting transfers between devices: 14.4 us -> 16.2 us  [swapped(): return lax.ppermute(array, axis, [(0, 1), (1, 0)])]
    all_gather x1, blocking collectives: 39 us -> 37.4 us  [body(): line = lax.all_gather(packed, 'z', axis=0, tiled=False)]
    all_gather x1, blocking collectives: 13.5 us -> 12.2 us  [body(): partners = lax.all_gather(kept, COL, axis=0, tiled=False)]
  transfers between devices with their start and end apart: 5 -> 5, of which waited for: 0 -> 1; matrix products, arithmetic and copies ran while one was open for 0% -> 0% of each run, Pallas kernels for 4% -> 4%
where the time goes in v7:
time: 126 us; the launch traced here: 125 us
  blocking collectives  76.9 us (61%)
  starting transfers between devices  20.6 us (16%)
  between operations  13.5 us (11%)
  Pallas kernels  12.5 us (10%)
  local copies, waits for them, and re-layouts  1.62 us (1%)
    all_gather x1, blocking collectives, body(): line = lax.all_gather(packed, 'z', axis=0, tiled=False)  37.4 us
    ppermute x3, starting transfers between devices, swapped(): return lax.ppermute(array, axis, [(0, 1), (1, 0)])  16.2 us
    all_to_all x1, blocking collectives, body(): plane = lax.all_to_all(slabs, PLANE, 0, 0, tiled=True)  15.1 us
    pallas_call x6, Pallas kernels, call(): pl.pallas_call(kernel, out_shape=shape, in_specs=specs, out_specs=out, sc...  12.5 us
    all_gather x1, blocking collectives, body(): partners = lax.all_gather(kept, COL, axis=0, tiled=False)  12.2 us
    all_to_all x1, blocking collectives, body(): summed = lax.all_to_all(projected, COL, 0, 0, tiled=True)  12.2 us
    all_to_all x1, starting transfers between devices, body(): arrived = lax.all_to_all(send, PLANE, 0, 0, tiled=True)  4.39 us
  transfers between devices with their start and end apart: 5, of which 1 were waited for; matrix products, arithmetic and copies ran while one was open for 0% of the time, Pallas kernels for 4%

profile of v7, /device:TPU:1, one launch (start us, length us, event | category | flops | bytes accessed | tf_op | source)
XLA Modules:
  0.0 125.4 jit_solution(13495165223618590305)
XLA Ops:
  6.5 0.0 copy-start.4
  6.5 0.0 copy-start
  6.5 0.0 copy-start.5
  6.5 0.0 all-gather.4.cloned.1.call-start
  6.5 2.2 %shard_map.64 = (bf16[8,2,16,512]{3,2,1,0:T(8,128)(2,1)S(1)}, bf16[192,128]{1,0:T(8,128)(2,1)S(1)}) custom-call(s32[2]{0:T(128)} %qsel.1, bf16[16,16,512]{2,1,0:T(8,128)(2,1)} %w.1, bf16[2,64,192]{2,1,0:T(8,128)(2,1)} %amps.1), custom_call_target="tpu_custom_call" | custom-call | tf_op jit(solution)/shard_map/pallas_call | solution.py:138
  8.8 15.1 %all_to_all.15 = bf16[8,2,16,512]{3,2,1,0:T(8,128)(2,1)} all-to-all(bf16[8,2,16,512]{3,2,1,0:T(8,128)(2,1)S(1)} %get-tuple-element.13), channel_id=1, replica_groups=mesh['y'=4,'xh'=2,'z'=16,'xl'=2,'c'=2] {'y','xh'}, dimensions={0} | all-to-all | bytes 524288 | tf_op jit(solution)/shard_map/all_to_all | solution.py:169
  23.9 0.0 all-gather.4.cloned.1.call-update
  23.9 37.4 %all-gather = bf16[3072,128]{1,0:T(8,128)(2,1)S(1)} all-gather(bf16[192,128]{1,0:T(8,128)(2,1)S(1)} %get-tuple-element.16), channel_id=2, replica_groups=mesh['y'=4,'xh'=2,'z'=16,'xl'=2,'c'=2] {'z'}, dimensions={0}, use_global_device_ids=true | all-gather | bytes 835584 | tf_op jit(solution)/shard_map/all_gather | solution.py:173
  61.2 1.9 %collective-permute-start.1 = (bf16[2,512,256]{2,1,0:T(8,128)(2,1)}, bf16[2,512,256]{2,1,0:T(8,128)(2,1)S(1)}, u32[]{:S(2)}, u32[]{:S(2)}) collective-permute-start(bf16[2,512,256]{2,1,0:T(8,128)(2,1)} %own_coeffs.1), channel_id=1, source_target_pairs={{0,2},{2,0},{1,3},{3,1},{4,6},{6,4},{5,7},{7,5},{8,10},{10,8},{9,1... | collective-permute-start | bytes 1572872 | tf_op jit(solution)/shard_map/ppermute | solution.py:134
  63.2 1.9 %shard_map.65 = bf16[8,2,192,128]{3,2,1,0:T(8,128)(2,1)} custom-call(s32[2,256]{1,0:T(2,128)} %partner.3, bf16[16,192,128]{2,1,0:T(8,128)(2,1)S(1)} %bitcast.3), custom_call_target="tpu_custom_call" | custom-call | tf_op jit(solution)/shard_map/pallas_call | solution.py:138
  65.0 4.4 %all-to-all-start.1 = ((bf16[8,2,192,128]{3,2,1,0:T(8,128)(2,1)}), bf16[8,2,192,128]{3,2,1,0:T(8,128)(2,1)S(1)}, u32[]{:S(2)}, u32[]{:S(2)}) async-start(bf16[8,2,192,128]{3,2,1,0:T(8,128)(2,1)} %shard_map.65), calls=%async_computation.1 | async-start | bytes 1572864 | tf_op jit(solution)/shard_map/all_to_all | solution.py:180
  69.4 0.0 copy-done
  69.4 11.3 %collective-permute-start = (bf16[2,512,256]{2,1,0:T(8,128)(2,1)S(1)}, bf16[2,512,256]{2,1,0:T(8,128)(2,1)S(1)}, u32[]{:S(2)}, u32[]{:S(2)}) collective-permute-start(bf16[2,512,256]{2,1,0:T(8,128)(2,1)S(1)} %copy-done), channel_id=1, source_target_pairs={{0,1},{1,0},{2,3},{3,2},{4,5},{5,4},{6,7},{7,6},{8,9},{9,8},{10,11... | collective-permute-start | bytes 1572872 | tf_op jit(solution)/shard_map/ppermute | solution.py:134
  80.7 0.0 collective-permute-done.1.refs_2_
  80.7 0.0 copy-start.1
  80.7 3.0 %collective-permute-start.2 = (bf16[2,512,256]{2,1,0:T(8,128)(2,1)S(1)}, bf16[2,512,256]{2,1,0:T(8,128)(2,1)S(1)}, u32[]{:S(2)}, u32[]{:S(2)}) collective-permute-start(bf16[2,512,256]{2,1,0:T(8,128)(2,1)S(1)} %collective-permute-done.1.refs_2_), channel_id=1, source_target_pairs={{0,1},{1,0},{2,3},{3,2},{4,5},{5,4},{6,7},{7,6},{8,9},{9,8},{10,11... | collective-permute-start | bytes 1572872 | tf_op jit(solution)/shard_map/ppermute | solution.py:134
  83.8 0.0 copy-done.4
  83.8 0.0 copy-done.5
  83.8 0.1 convert_multiply_fusion.base
  83.9 0.2 all-to-all-done.1.arrived
  84.1 0.7 shard_map.66
  84.8 12.2 %all-gather.1 = bf16[8,192,128]{2,1,0:T(8,128)(2,1)S(1)} all-gather(bf16[2,192,128]{2,1,0:T(8,128)(2,1)S(1)} %shard_map.66), channel_id=3, replica_groups=mesh['y'=4,'xh'=2,'z'=16,'xl'=2,'c'=2] {'xl','c'}, dimensions={0}, use_global_device_ids=true | all-gather | bytes 491520 | tf_op jit(solution)/shard_map/all_gather | solution.py:182
  97.0 0.0 collective-permute-done.refs_1_
  97.0 0.0 collective-permute-done.2.refs_3_
  97.1 0.0 copy-done.1
  97.1 0.8 copy-done.2
  97.9 0.8 copy-done.3
  98.7 2.9 %shard_map.67.dens = bf16[4,2,384,512]{3,2,1,0:T(8,128)(2,1)S(1)} custom-call(bf16[4,2,192,128]{3,2,1,0:T(8,128)(2,1)S(1)} %bitcast.4, bf16[2,512,256]{2,1,0:T(8,128)(2,1)} %own_coeffs.1, bf16[2,512,256]{2,1,0:T(8,128)(2,1)} %copy-done.2, bf16[2,512,256]{2,1,0:T(8,128)(2,1)} %copy-done.1, bf16[2,512,256]{2,1,0:T(8,128)(2,1)} %copy-done.3), custom_call_target="tpu_custom_call" | custom-call | tf_op jit(solution)/shard_map/pallas_call | solution.py:138
  101.5 0.0 all-gather.4.cloned.1.call-done.w
  101.6 4.1 %shard_map.68 = bf16[4,192,128]{2,1,0:T(8,128)(2,1)S(1)} custom-call(bf16[16,4,2,2,16,512]{5,4,3,2,1,0:T(8,128)(2,1)} %all-gather.4.cloned.1.call-done.w, bf16[4,2,384,512]{3,2,1,0:T(8,128)(2,1)S(1)} %shard_map.67.dens, bf16[2,512,256]{2,1,0:T(8,128)(2,1)} %own_coeffs.1), custom_call_target="tpu_custom_call" | custom-call | tf_op jit(solution)/shard_map/pallas_call | solution.py:138
  105.6 12.2 %all_to_all.16.arrived = bf16[4,192,128]{2,1,0:T(8,128)(2,1)S(1)} all-to-all(bf16[4,192,128]{2,1,0:T(8,128)(2,1)S(1)} %shard_map.68), channel_id=1, replica_groups=mesh['y'=4,'xh'=2,'z'=16,'xl'=2,'c'=2] {'xl','c'}, dimensions={0} | all-to-all | bytes 393216 | tf_op jit(solution)/shard_map/all_to_all | solution.py:198
  117.8 0.7 shard_map.69
  (2 shorter events, 0.0 us)
Async XLA Ops:
  6.5 77.3 %copy-start.4 = (bf16[2,64,192]{2,1,0:T(8,128)(2,1)S(1)}, bf16[2,64,192]{2,1,0:T(8,128)(2,1)}, u32[]{:S(2)}) copy-start(bf16[2,64,192]{2,1,0:T(8,128)(2,1)} %amps.1) | copy-start | bytes 147460
  6.5 62.9 %copy-start = (bf16[2,512,256]{2,1,0:T(8,128)(2,1)S(1)}, bf16[2,512,256]{2,1,0:T(8,128)(2,1)}, u32[]{:S(2)}) copy-start(bf16[2,512,256]{2,1,0:T(8,128)(2,1)} %own_coeffs.1) | copy-start | bytes 1572868
  6.5 77.3 %copy-start.5 = (f32[2,64]{1,0:T(2,128)S(1)}, f32[2,64]{1,0:T(2,128)}, u32[]{:S(2)}) copy-start(f32[2,64]{1,0:T(2,128)} %param.9) | copy-start | bytes 1540
  6.5 95.0 %all-gather.4.cloned.1.call-start = ((), (), s32[]{:S(2)}) async-start(), calls=%async_computation.3 | async-start | bytes 4456448 | tf_op jit(solution)/shard_map/all_gather | solution.py:171
  61.2 19.5 %collective-permute-start.1 = (bf16[2,512,256]{2,1,0:T(8,128)(2,1)}, bf16[2,512,256]{2,1,0:T(8,128)(2,1)S(1)}, u32[]{:S(2)}, u32[]{:S(2)}) collective-permute-start(bf16[2,512,256]{2,1,0:T(8,128)(2,1)} %own_coeffs.1), channel_id=1, source_target_pairs={{0,2},{2,0},{1,3},{3,1},{4,6},{6,4},{5,7},{7,5},{8,10},{10,8},{9,1... | collective-permute-start | bytes 1572872 | tf_op jit(solution)/shard_map/ppermute | solution.py:134
  65.0 19.1 %all-to-all-start.1 = ((bf16[8,2,192,128]{3,2,1,0:T(8,128)(2,1)}), bf16[8,2,192,128]{3,2,1,0:T(8,128)(2,1)S(1)}, u32[]{:S(2)}, u32[]{:S(2)}) async-start(bf16[8,2,192,128]{3,2,1,0:T(8,128)(2,1)} %shard_map.65), calls=%async_computation.1 | async-start | bytes 1572864 | tf_op jit(solution)/shard_map/all_to_all | solution.py:180
  69.4 27.6 %collective-permute-start = (bf16[2,512,256]{2,1,0:T(8,128)(2,1)S(1)}, bf16[2,512,256]{2,1,0:T(8,128)(2,1)S(1)}, u32[]{:S(2)}, u32[]{:S(2)}) collective-permute-start(bf16[2,512,256]{2,1,0:T(8,128)(2,1)S(1)} %copy-done), channel_id=1, source_target_pairs={{0,1},{1,0},{2,3},{3,2},{4,5},{5,4},{6,7},{7,6},{8,9},{9,8},{10,11... | collective-permute-start | bytes 1572872 | tf_op jit(solution)/shard_map/ppermute | solution.py:134
  80.7 16.3 %copy-start.1 = (bf16[2,512,256]{2,1,0:T(8,128)(2,1)}, bf16[2,512,256]{2,1,0:T(8,128)(2,1)S(1)}, u32[]{:S(2)}) copy-start(bf16[2,512,256]{2,1,0:T(8,128)(2,1)S(1)} %collective-permute-done.1.refs_2_) | copy-start | bytes 1572868
  80.7 16.3 %collective-permute-start.2 = (bf16[2,512,256]{2,1,0:T(8,128)(2,1)S(1)}, bf16[2,512,256]{2,1,0:T(8,128)(2,1)S(1)}, u32[]{:S(2)}, u32[]{:S(2)}) collective-permute-start(bf16[2,512,256]{2,1,0:T(8,128)(2,1)S(1)} %collective-permute-done.1.refs_2_), channel_id=1, source_target_pairs={{0,1},{1,0},{2,3},{3,2},{4,5},{5,4},{6,7},{7,6},{8,9},{9,8},{10,11... | collective-permute-start | bytes 1572872 | tf_op jit(solution)/shard_map/ppermute | solution.py:134
  97.0 0.8 copy-start.2
  97.9 0.8 copy-start.3
Sparse Core Ops, SparseCore 0:
  24.0 74.2 all-gather.3

commit v8 on v7

--- a/solution.py
+++ b/solution.py
@@ -98,7 +98,7 @@
 def screen_kernel(w, dens, own_coeffs, out, rows, coeffs, arrived, ready):
     c = lax.axis_index(COL)
     steps = [(j, i) for j in range(2) for i in range(N_COL)]
-    copies = {(j, i): pltpu.make_async_copy(w.at[:, c ^ i, :, j], rows.at[i, j], arrived.at[i, j]) for j, i in steps}
+    copies = {(j, i): pltpu.make_async_copy(w.at[:, :, c ^ i, j], rows.at[i, j], arrived.at[i, j]) for j, i in steps}
     for step in steps:
         copies[step].start()
     last = pltpu.make_async_copy(own_coeffs, coeffs, ready)
@@ -166,9 +166,9 @@
             pltpu.VMEM((2, 64, VEC), jnp.bfloat16), pltpu.SemaphoreType.DMA((8, 2)), pltpu.SemaphoreType.DMA,
         ],
     )
-    plane = lax.all_to_all(slabs, PLANE, 0, 0, tiled=True)
+    plane = lax.all_to_all(slabs, ("xh", "y"), 0, 0, tiled=True)
     plane, packed = lax.optimization_barrier((plane, packed))
-    rows = lax.all_gather(plane.reshape(N_Y, N_XH, 2, 16, 512), "z", axis=0, tiled=False)
+    rows = lax.all_gather(plane.reshape(N_XH, N_Y, 2, 16, 512), "z", axis=0, tiled=False)
 
     line = lax.all_gather(packed, "z", axis=0, tiled=False)
     line, coeffs = lax.optimization_barrier((line, isdf_coeffs))

time: 126 us -> 126 us (level)
  no operation moved by 1% of the time
where the time goes in v8:
time: 126 us
  blocking collectives  77 us (61%)
  starting transfers between devices  20.6 us (16%)
  between operations  13.5 us (11%)
  Pallas kernels  12.5 us (10%)
  local copies, waits for them, and re-layouts  1.62 us (1%)
    all_gather x1, blocking collectives, body(): line = lax.all_gather(packed, 'z', axis=0, tiled=False)  37.2 us
    ppermute x3, starting transfers between devices, swapped(): return lax.ppermute(array, axis, [(0, 1), (1, 0)])  16.5 us
    all_to_all x1, blocking collectives, body(): plane = lax.all_to_all(slabs, ('xh', 'y'), 0, 0, tiled=True)  15.1 us
    pallas_call x6, Pallas kernels, call(): pl.pallas_call(kernel, out_shape=shape, in_specs=specs, out_specs=out, sc...  12.5 us
    all_gather x1, blocking collectives, body(): partners = lax.all_gather(kept, COL, axis=0, tiled=False)  12.4 us
    all_to_all x1, blocking collectives, body(): summed = lax.all_to_all(projected, COL, 0, 0, tiled=True)  12.3 us
    all_to_all x1, starting transfers between devices, body(): arrived = lax.all_to_all(send, PLANE, 0, 0, tiled=True)  4.17 us
  transfers between devices with their start and end apart: 5, of which 1 were waited for; matrix products, arithmetic and copies ran while one was open for 0% of the time, Pallas kernels for 4%

profile of v8, /device:TPU:1, one launch (start us, length us, event | category | flops | bytes accessed | tf_op | source)
XLA Modules:
  0.0 125.7 jit_solution(12122358938627400540)
XLA Ops:
  6.5 0.0 copy-start.4
  6.5 0.0 copy-start
  6.5 0.0 copy-start.5
  6.5 0.0 all-gather.4.cloned.1.call-start
  6.5 2.2 %shard_map.64 = (bf16[8,2,16,512]{3,2,1,0:T(8,128)(2,1)S(1)}, bf16[192,128]{1,0:T(8,128)(2,1)S(1)}) custom-call(s32[2]{0:T(128)} %qsel.1, bf16[16,16,512]{2,1,0:T(8,128)(2,1)} %w.1, bf16[2,64,192]{2,1,0:T(8,128)(2,1)} %amps.1), custom_call_target="tpu_custom_call" | custom-call | tf_op jit(solution)/shard_map/pallas_call | solution.py:138
  8.8 15.1 %all_to_all.15 = bf16[8,2,16,512]{3,2,1,0:T(8,128)(2,1)} all-to-all(bf16[8,2,16,512]{3,2,1,0:T(8,128)(2,1)S(1)} %get-tuple-element.13), channel_id=1, replica_groups=mesh['y'=4,'xh'=2,'z'=16,'xl'=2,'c'=2] {'xh','y'}, dimensions={0} | all-to-all | bytes 524288 | tf_op jit(solution)/shard_map/all_to_all | solution.py:169
  23.9 0.0 all-gather.4.cloned.1.call-update
  23.9 37.2 %all-gather = bf16[3072,128]{1,0:T(8,128)(2,1)S(1)} all-gather(bf16[192,128]{1,0:T(8,128)(2,1)S(1)} %get-tuple-element.16), channel_id=2, replica_groups=mesh['y'=4,'xh'=2,'z'=16,'xl'=2,'c'=2] {'z'}, dimensions={0}, use_global_device_ids=true | all-gather | bytes 835584 | tf_op jit(solution)/shard_map/all_gather | solution.py:173
  61.1 2.3 %collective-permute-start.1 = (bf16[2,512,256]{2,1,0:T(8,128)(2,1)}, bf16[2,512,256]{2,1,0:T(8,128)(2,1)S(1)}, u32[]{:S(2)}, u32[]{:S(2)}) collective-permute-start(bf16[2,512,256]{2,1,0:T(8,128)(2,1)} %own_coeffs.1), channel_id=1, source_target_pairs={{0,2},{2,0},{1,3},{3,1},{4,6},{6,4},{5,7},{7,5},{8,10},{10,8},{9,1... | collective-permute-start | bytes 1572872 | tf_op jit(solution)/shard_map/ppermute | solution.py:134
  63.4 1.9 %shard_map.65 = bf16[8,2,192,128]{3,2,1,0:T(8,128)(2,1)} custom-call(s32[2,256]{1,0:T(2,128)} %partner.3, bf16[16,192,128]{2,1,0:T(8,128)(2,1)S(1)} %bitcast.3), custom_call_target="tpu_custom_call" | custom-call | tf_op jit(solution)/shard_map/pallas_call | solution.py:138
  65.2 4.2 %all-to-all-start.1 = ((bf16[8,2,192,128]{3,2,1,0:T(8,128)(2,1)}), bf16[8,2,192,128]{3,2,1,0:T(8,128)(2,1)S(1)}, u32[]{:S(2)}, u32[]{:S(2)}) async-start(bf16[8,2,192,128]{3,2,1,0:T(8,128)(2,1)} %shard_map.65), calls=%async_computation.1 | async-start | bytes 1572864 | tf_op jit(solution)/shard_map/all_to_all | solution.py:180
  69.4 0.0 copy-done
  69.4 11.4 %collective-permute-start = (bf16[2,512,256]{2,1,0:T(8,128)(2,1)S(1)}, bf16[2,512,256]{2,1,0:T(8,128)(2,1)S(1)}, u32[]{:S(2)}, u32[]{:S(2)}) collective-permute-start(bf16[2,512,256]{2,1,0:T(8,128)(2,1)S(1)} %copy-done), channel_id=1, source_target_pairs={{0,1},{1,0},{2,3},{3,2},{4,5},{5,4},{6,7},{7,6},{8,9},{9,8},{10,11... | collective-permute-start | bytes 1572872 | tf_op jit(solution)/shard_map/ppermute | solution.py:134
  80.9 0.0 collective-permute-done.1.refs_2_
  80.9 0.0 copy-start.1
  80.9 2.8 %collective-permute-start.2 = (bf16[2,512,256]{2,1,0:T(8,128)(2,1)S(1)}, bf16[2,512,256]{2,1,0:T(8,128)(2,1)S(1)}, u32[]{:S(2)}, u32[]{:S(2)}) collective-permute-start(bf16[2,512,256]{2,1,0:T(8,128)(2,1)S(1)} %collective-permute-done.1.refs_2_), channel_id=1, source_target_pairs={{0,1},{1,0},{2,3},{3,2},{4,5},{5,4},{6,7},{7,6},{8,9},{9,8},{10,11... | collective-permute-start | bytes 1572872 | tf_op jit(solution)/shard_map/ppermute | solution.py:134
  83.7 0.0 copy-done.4
  83.7 0.0 copy-done.5
  83.7 0.1 convert_multiply_fusion.base
  83.8 0.3 all-to-all-done.1.arrived
  84.1 0.7 shard_map.66
  84.8 12.4 %all-gather.1 = bf16[8,192,128]{2,1,0:T(8,128)(2,1)S(1)} all-gather(bf16[2,192,128]{2,1,0:T(8,128)(2,1)S(1)} %shard_map.66), channel_id=3, replica_groups=mesh['y'=4,'xh'=2,'z'=16,'xl'=2,'c'=2] {'xl','c'}, dimensions={0}, use_global_device_ids=true | all-gather | bytes 491520 | tf_op jit(solution)/shard_map/all_gather | solution.py:182
  97.2 0.0 collective-permute-done.refs_1_
  97.2 0.0 collective-permute-done.2.refs_3_
  97.2 0.0 copy-done.1
  97.2 0.8 copy-done.2
  98.0 0.8 copy-done.3
  98.8 2.9 %shard_map.67.dens = bf16[4,2,384,512]{3,2,1,0:T(8,128)(2,1)S(1)} custom-call(bf16[4,2,192,128]{3,2,1,0:T(8,128)(2,1)S(1)} %bitcast.4, bf16[2,512,256]{2,1,0:T(8,128)(2,1)} %own_coeffs.1, bf16[2,512,256]{2,1,0:T(8,128)(2,1)} %copy-done.2, bf16[2,512,256]{2,1,0:T(8,128)(2,1)} %copy-done.1, bf16[2,512,256]{2,1,0:T(8,128)(2,1)} %copy-done.3), custom_call_target="tpu_custom_call" | custom-call | tf_op jit(solution)/shard_map/pallas_call | solution.py:138
  101.7 0.0 all-gather.4.cloned.1.call-done.w
  101.7 4.0 %shard_map.68 = bf16[4,192,128]{2,1,0:T(8,128)(2,1)S(1)} custom-call(bf16[16,2,4,2,16,512]{5,4,3,2,1,0:T(8,128)(2,1)} %all-gather.4.cloned.1.call-done.w, bf16[4,2,384,512]{3,2,1,0:T(8,128)(2,1)S(1)} %shard_map.67.dens, bf16[2,512,256]{2,1,0:T(8,128)(2,1)} %own_coeffs.1), custom_call_target="tpu_custom_call" | custom-call | tf_op jit(solution)/shard_map/pallas_call | solution.py:138
  105.8 12.3 %all_to_all.16.arrived = bf16[4,192,128]{2,1,0:T(8,128)(2,1)S(1)} all-to-all(bf16[4,192,128]{2,1,0:T(8,128)(2,1)S(1)} %shard_map.68), channel_id=1, replica_groups=mesh['y'=4,'xh'=2,'z'=16,'xl'=2,'c'=2] {'xl','c'}, dimensions={0} | all-to-all | bytes 393216 | tf_op jit(solution)/shard_map/all_to_all | solution.py:198
  118.1 0.7 shard_map.69
  (2 shorter events, 0.0 us)
Async XLA Ops:
  6.5 77.1 %copy-start.4 = (bf16[2,64,192]{2,1,0:T(8,128)(2,1)S(1)}, bf16[2,64,192]{2,1,0:T(8,128)(2,1)}, u32[]{:S(2)}) copy-start(bf16[2,64,192]{2,1,0:T(8,128)(2,1)} %amps.1) | copy-start | bytes 147460
  6.5 62.9 %copy-start = (bf16[2,512,256]{2,1,0:T(8,128)(2,1)S(1)}, bf16[2,512,256]{2,1,0:T(8,128)(2,1)}, u32[]{:S(2)}) copy-start(bf16[2,512,256]{2,1,0:T(8,128)(2,1)} %own_coeffs.1) | copy-start | bytes 1572868
  6.5 77.1 %copy-start.5 = (f32[2,64]{1,0:T(2,128)S(1)}, f32[2,64]{1,0:T(2,128)}, u32[]{:S(2)}) copy-start(f32[2,64]{1,0:T(2,128)} %param.9) | copy-start | bytes 1540
  6.5 95.2 %all-gather.4.cloned.1.call-start = ((), (), s32[]{:S(2)}) async-start(), calls=%async_computation.3 | async-start | bytes 4456448 | tf_op jit(solution)/shard_map/all_gather | solution.py:171
  61.1 19.8 %collective-permute-start.1 = (bf16[2,512,256]{2,1,0:T(8,128)(2,1)}, bf16[2,512,256]{2,1,0:T(8,128)(2,1)S(1)}, u32[]{:S(2)}, u32[]{:S(2)}) collective-permute-start(bf16[2,512,256]{2,1,0:T(8,128)(2,1)} %own_coeffs.1), channel_id=1, source_target_pairs={{0,2},{2,0},{1,3},{3,1},{4,6},{6,4},{5,7},{7,5},{8,10},{10,8},{9,1... | collective-permute-start | bytes 1572872 | tf_op jit(solution)/shard_map/ppermute | solution.py:134
  65.2 18.8 %all-to-all-start.1 = ((bf16[8,2,192,128]{3,2,1,0:T(8,128)(2,1)}), bf16[8,2,192,128]{3,2,1,0:T(8,128)(2,1)S(1)}, u32[]{:S(2)}, u32[]{:S(2)}) async-start(bf16[8,2,192,128]{3,2,1,0:T(8,128)(2,1)} %shard_map.65), calls=%async_computation.1 | async-start | bytes 1572864 | tf_op jit(solution)/shard_map/all_to_all | solution.py:180
  69.4 27.8 %collective-permute-start = (bf16[2,512,256]{2,1,0:T(8,128)(2,1)S(1)}, bf16[2,512,256]{2,1,0:T(8,128)(2,1)S(1)}, u32[]{:S(2)}, u32[]{:S(2)}) collective-permute-start(bf16[2,512,256]{2,1,0:T(8,128)(2,1)S(1)} %copy-done), channel_id=1, source_target_pairs={{0,1},{1,0},{2,3},{3,2},{4,5},{5,4},{6,7},{7,6},{8,9},{9,8},{10,11... | collective-permute-start | bytes 1572872 | tf_op jit(solution)/shard_map/ppermute | solution.py:134
  80.9 16.3 %copy-start.1 = (bf16[2,512,256]{2,1,0:T(8,128)(2,1)}, bf16[2,512,256]{2,1,0:T(8,128)(2,1)S(1)}, u32[]{:S(2)}) copy-start(bf16[2,512,256]{2,1,0:T(8,128)(2,1)S(1)} %collective-permute-done.1.refs_2_) | copy-start | bytes 1572868
  80.9 16.3 %collective-permute-start.2 = (bf16[2,512,256]{2,1,0:T(8,128)(2,1)S(1)}, bf16[2,512,256]{2,1,0:T(8,128)(2,1)S(1)}, u32[]{:S(2)}, u32[]{:S(2)}) collective-permute-start(bf16[2,512,256]{2,1,0:T(8,128)(2,1)S(1)} %collective-permute-done.1.refs_2_), channel_id=1, source_target_pairs={{0,1},{1,0},{2,3},{3,2},{4,5},{5,4},{6,7},{7,6},{8,9},{9,8},{10,11... | collective-permute-start | bytes 1572872 | tf_op jit(solution)/shard_map/ppermute | solution.py:134
  97.2 0.8 copy-start.2
  98.0 0.8 copy-start.3
Sparse Core Ops, SparseCore 0:
  24.0 73.9 all-gather.3
